TPU v7x, 128 devices: a whole 4x4x4 slice. The times are simulated.
128 devices in a mesh: rows: 128 (over x, z, y, core).
Axes of the slice: x: 4, y: 4, z: 4, core: 2. Of those that a mesh axis runs over, the one named last changes fastest.
Arguments:
- history: float32 [32, 2048, 4096], P(None, 'rows'), may hold values from 0.2 to 1.8, as said below
- source: float32 [2048, 4096], P('rows'), may hold values from 0.5 to 2, as said below
- diffusivity: float32 [2048, 4096], P('rows'), may hold values from 0.5 to 2, as said below
- target: float32 [2048, 4096], P('rows'), may hold values from -0.5 to 2.5, as said below
Outputs:
- update: float32 [2048, 4096], P('rows')
- totals: float32 [2], replicated
Inputs may be any that keep to these rules, and one draw needn't show every extreme that they name: `history`: every level is a field between 0.2 and 1.8, smooth with a small cell-by-cell variation. `source`: a positive field between 0.5 and 2. `diffusivity`: a positive field between 0.5 and 2, smooth with a small cell-by-cell variation. `target`: a field between -0.5 and 2.5, smooth with a small cell-by-cell variation.
All inputs are finite; a program needn't handle non-finite values.
Results may differ from a plain program's by a relative error of at most 0.0003.
Values sent between devices are 32-bit elements; how exact they have to be, the bound alone decides.
No kernel may reach another device: no remote copies, remote signals or barrier semaphores. Data moves between devices by JAX's collectives and lax.ppermute only.
A program may use at most 128 MiB of HBM per device.

v0:
```python
import jax
import jax.numpy as jnp
from jax import lax
from jax.sharding import Mesh
from jax.sharding import PartitionSpec as P

STIFF = 1024
ROWS = ("rows_0", "rows_1", "rows_2", "rows_3")


frac_order = 0.6


def shifted(value, axis, steps):
    count = lax.axis_size(axis)
    leading, last = (max(0, -steps), min(count, count - steps))
    return lax.ppermute(value, axis, [(source, source + steps) for source in range(leading, last)])


def over_axes(x, axes):
    for axis in axes:
        x = lax.psum(x, axis)
    return x


def memory_weights(levels):
    moments = jnp.arange(levels + 1, dtype=jnp.float32)
    powered = moments ** (1.0 - frac_order)
    decay_terms = powered[1:] - powered[:-1]
    padding = jnp.zeros((1,), jnp.float32)
    return jnp.concatenate([decay_terms[1:], padding]) - jnp.concatenate([padding, decay_terms[1:]])


def take_from(array_in, stride, fill_value, along, before):
    length = array_in.shape[along]
    pad_shape = list(array_in.shape)
    pad_shape[along] = stride
    filler = jnp.full(pad_shape, fill_value, array_in.dtype)
    if before:
        kept = lax.slice_in_dim(array_in, 0, length - stride, 1, along)
        return jnp.concatenate([filler, kept], along)
    kept = lax.slice_in_dim(array_in, stride, length, 1, along)
    return jnp.concatenate([kept, filler], along)


def cyclic_solve(along, sub_diag, main_diag, sup_diag, right_sides):
    length = main_diag.shape[along]
    level_total = (length - 1).bit_length()
    sub_now, main_now, sup_now, rights_now = (sub_diag, main_diag, sup_diag, tuple(right_sides))
    for level_at in range(level_total):
        stride = 1 << level_at
        sub_up = take_from(sub_now, stride, 0.0, along, True)
        main_up = take_from(main_now, stride, 1.0, along, True)
        sup_up = take_from(sup_now, stride, 0.0, along, True)
        sub_down = take_from(sub_now, stride, 0.0, along, False)
        main_down = take_from(main_now, stride, 1.0, along, False)
        sup_down = take_from(sup_now, stride, 0.0, along, False)
        factor_up = sub_now / main_up
        factor_down = sup_now / main_down
        new_main = main_now - factor_up * sup_up - factor_down * sub_down
        new_sub = -factor_up * sub_up
        new_sup = -factor_down * sup_down
        rights_now = tuple(
            (
                operand
                - factor_up * take_from(operand, stride, 0.0, along, True)
                - factor_down * take_from(operand, stride, 0.0, along, False)
                for operand in rights_now
            )
        )
        sub_now, main_now, sup_now = (new_sub, new_main, new_sup)
    return tuple((operand / main_now for operand in rights_now))


def body(history, source, diffusivity, target):
    level_count = history.shape[0]
    local_rows = diffusivity.shape[0]
    width_cells = diffusivity.shape[1]
    stiffness = float(STIFF)
    weights = memory_weights(level_count)
    memory = jnp.dot(
        weights,
        history.reshape(level_count, local_rows * width_cells),
        precision=lax.Precision.HIGHEST,
    ).reshape(local_rows, width_cells)
    driven = history[0] - memory + source
    coupling = -stiffness * diffusivity
    main_band = 1.0 + 2.0 * stiffness * diffusivity
    column_pos = lax.broadcasted_iota(jnp.int32, diffusivity.shape, 1)
    sub_x = jnp.where(column_pos == 0, 0.0, coupling)
    sup_x = jnp.where(column_pos == width_cells - 1, 0.0, coupling)
    (swept,) = cyclic_solve(1, sub_x, main_band, sup_x, (driven,))
    device_count = lax.axis_size(ROWS)
    total_rows = device_count * local_rows
    row_pos = lax.axis_index(ROWS) * local_rows + lax.broadcasted_iota(
        jnp.int32, diffusivity.shape, 0
    )
    sub_y = jnp.where(row_pos == 0, 0.0, coupling)
    sup_y = jnp.where(row_pos == total_rows - 1, 0.0, coupling)
    inner_rows = local_rows - 1
    inner_pos = lax.broadcasted_iota(jnp.int32, (inner_rows, width_cells), 0)
    cut_sub = jnp.where(inner_pos == 0, 0.0, sub_y[:inner_rows])
    cut_sup = jnp.where(inner_pos == inner_rows - 1, 0.0, sup_y[:inner_rows])
    unit_top = jnp.where(inner_pos == 0, 1.0, 0.0)
    unit_bottom = jnp.where(inner_pos == inner_rows - 1, 1.0, 0.0)
    partial_value, top_spike, bottom_spike = cyclic_solve(
        0, cut_sub, main_band[:inner_rows], cut_sup, (swept[:inner_rows], unit_top, unit_bottom)
    )
    from_above = sub_y[0] * top_spike
    from_below = sup_y[inner_rows - 1] * bottom_spike
    leading = jnp.stack([partial_value[0], from_above[0], from_below[0]])
    next_rows = shifted(leading, ROWS, -1)
    next_partial = next_rows[0]
    next_above = next_rows[1]
    next_below = next_rows[2]
    edge_sub = sub_y[inner_rows]
    edge_sup = sup_y[inner_rows]
    tip_sub = -edge_sub * from_above[inner_rows - 1]
    tip_main = main_band[inner_rows] - edge_sub * from_below[inner_rows - 1] - edge_sup * next_above
    tip_sup = -edge_sup * next_below
    tip_right = (
        swept[inner_rows] - edge_sub * partial_value[inner_rows - 1] - edge_sup * next_partial
    )
    tip_rows = jnp.stack([tip_sub, tip_main, tip_sup, tip_right])[None]
    spread = lax.all_to_all(tip_rows, ROWS, split_axis=2, concat_axis=0, tiled=True)
    (solved_cols,) = cyclic_solve(0, spread[:, 0], spread[:, 1], spread[:, 2], (spread[:, 3],))
    above_cols = jnp.concatenate([jnp.zeros_like(solved_cols[:1]), solved_cols[:-1]], 0)
    paired = jnp.stack([solved_cols, above_cols], 1)
    returned = lax.all_to_all(paired, ROWS, split_axis=0, concat_axis=2, tiled=True)
    own_tip = returned[0, 0]
    prev_tip = returned[0, 1]
    interior = partial_value - from_above * prev_tip - from_below * own_tip
    update = jnp.concatenate([interior, own_tip[None]], 0)
    mass_sum, error_sum = (
        over_axes(jnp.sum(update), ROWS),
        over_axes(jnp.sum((update - target) ** 2), ROWS),
    )
    cell_count = float(total_rows * width_cells)
    return (update, jnp.stack([mass_sum / cell_count, error_sum / cell_count]))


def solution(mesh):
    split = Mesh(mesh.devices.reshape(4, 4, 4, 2), ("rows_0", "rows_1", "rows_2", "rows_3"))
    return jax.shard_map(
        body,
        mesh=split,
        in_specs=(P(None, ROWS, None), P(ROWS, None), P(ROWS, None), P(ROWS, None)),
        out_specs=(P(ROWS, None), P()),
        check_vma=False,
    )
```

profile of v0, /device:TPU:1, one launch (start us, length us, event | category | flops | bytes accessed | tf_op | source)
XLA Modules:
  0.0 142.8 jit_solution(11704171504635440177)
XLA Ops:
  0.9 1.0 multiply_select_fusion.2
  1.9 12.6 %fusion = f32[1,16,4096]{2,0,1:T(1,128)S(1)} fusion(f32[1]{0:T(128)} %constant.19.clone.1, f32[31]{0:T(128)S(1)} %slice.722, f32[4,8,16,4096]{3,2,1,0:T(8,128)} %bitcast.94), kind=kOutput, calls=%fused_computation | convolution fusion | flops 25165920 | bytes 8650880 | tf_op jit(solution)/shard_map/dot_general | solution.py:81
  14.5 1.1 fusion.5
  15.8 0.9 fusion.87
  16.7 0.3 multiply_subtract_fusion.32
  17.3 1.3 multiply_subtract_fusion.31
  19.4 0.3 multiply_subtract_fusion.29
  20.6 0.3 multiply_subtract_fusion.27
  21.7 0.3 multiply_subtract_fusion.25
  22.8 0.3 multiply_subtract_fusion.23
  24.0 0.3 multiply_subtract_fusion.21
  28.5 0.3 multiply_subtract_fusion.9
  29.0 0.3 multiply_subtract_fusion.4
  29.9 3.3 %collective-permute-start = (f32[3,4096]{1,0:T(4,128)S(1)}, f32[3,4096]{1,0:T(4,128)S(1)}, u32[]{:S(2)}, u32[]{:S(2)}) collective-permute-start(f32[3,4096]{1,0:T(4,128)S(1)} %pad_maximum_fusion.2), channel_id=1, source_target_pairs={{1,0},{2,1},{3,2},{4,3},{5,4},{6,5},{7,6},{8,7},{9,8},{10,9},{11,1... | collective-permute-start | bytes 147464 | tf_op jit(solution)/shard_map/ppermute | solution.py:17
  33.2 3.2 %collective-permute-done = f32[3,4096]{1,0:T(4,128)S(1)} collective-permute-done((f32[3,4096]{1,0:T(4,128)S(1)}, f32[3,4096]{1,0:T(4,128)S(1)}, u32[]{:S(2)}, u32[]{:S(2)}) %collective-permute-start) | collective-permute-done | bytes 49184 | tf_op jit(solution)/shard_map/ppermute | solution.py:17
  36.6 0.6 copy.37
  37.3 0.5 broadcast.485
  37.8 19.6 %reduce.3 = f32[4096,4]{1,0:T(8,128)} reduce(f32[4096,1,4]{2,1,0:T(1,128)S(1)} %bitcast.95, f32[]{:T(128)} %broadcast.485), dimensions={1}, to_apply=%bitcast.86.reduce_sub_computation | reduce | bytes 131076
  57.4 3.4 %reshape.22 = f32[128,1,128]{2,1,0:T(1,128)S(1)} reshape(f32[4096,4]{1,0:T(8,128)} %reduce.3) | data formatting | bytes 131072
  60.8 23.4 %all_to_all.36 = f32[128,1,128]{2,1,0:T(1,128)S(1)} all-to-all(f32[128,1,128]{2,1,0:T(1,128)S(1)} %reshape.22), channel_id=1, replica_groups=mesh['rows_0'=4,'rows_1'=4,'rows_2'=4,'rows_3'=2] {'rows_0','rows_1','ro..., dimensions={0} | all-to-all | bytes 131072 | tf_op jit(solution)/shard_map/all_to_all | solution.py:125
  84.1 0.8 reduce.4
  85.0 3.4 %reshape.23 = f32[4096,1,4]{2,1,0:T(1,128)S(1)} reshape(f32[128,128]{1,0:T(8,128)S(1)} %reduce.4) | data formatting | bytes 131072
  88.3 1.0 copy.43
  90.7 14.5 %all_to_all.37 = f32[128,2,32]{2,1,0:T(2,128)S(1)} all-to-all(f32[128,2,32]{2,1,0:T(2,128)S(1)} %copy.39), channel_id=1, replica_groups=mesh['rows_0'=4,'rows_1'=4,'rows_2'=4,'rows_3'=2] {'rows_0','rows_1','ro..., dimensions={0} | all-to-all | bytes 65536 | tf_op jit(solution)/shard_map/all_to_all | solution.py:129
  105.4 0.6 slice_reduce_fusion
  106.0 0.7 fusion.26
  108.0 1.3 multiply_reduce_fusion
  109.3 7.5 %all-reduce.197 = (f32[]{:T(128)}, f32[]{:T(128)}) all-reduce(f32[]{:T(128)} %get-tuple-element.16, f32[]{:T(128)S(6)} %reduce_sum.28), channel_id=1, replica_groups=mesh['rows_0'=4,'rows_1'=4,'rows_2'=4,'rows_3'=2] {'rows_0'}, use_global_device_ids=true, to_apply=%region_7.8 | all-reduce | flops 2 | bytes 16 | tf_op jit(solution)/shard_map/psum | solution.py:22
  116.8 7.4 %all-reduce.196 = (f32[]{:T(128)}, f32[]{:T(128)}) all-reduce(f32[]{:T(128)} %get-tuple-element.10, f32[]{:T(128)} %get-tuple-element.11), channel_id=1, replica_groups=mesh['rows_0'=4,'rows_1'=4,'rows_2'=4,'rows_3'=2] {'rows_1'}, use_global_device_ids=true, to_apply=%region_8.9 | all-reduce | flops 2 | bytes 16 | tf_op jit(solution)/shard_map/psum | solution.py:22
  124.2 7.5 %all-reduce.195 = (f32[]{:T(128)}, f32[]{:T(128)}) all-reduce(f32[]{:T(128)} %get-tuple-element.8, f32[]{:T(128)} %get-tuple-element.9), channel_id=1, replica_groups=mesh['rows_0'=4,'rows_1'=4,'rows_2'=4,'rows_3'=2] {'rows_2'}, use_global_device_ids=true, to_apply=%region_9.10 | all-reduce | flops 2 | bytes 16 | tf_op jit(solution)/shard_map/psum | solution.py:22
  131.7 9.3 %all-reduce.198 = (f32[]{:T(128)}, f32[]{:T(128)}) all-reduce(f32[]{:T(128)} %get-tuple-element.6, f32[]{:T(128)} %get-tuple-element.7), channel_id=1, replica_groups=mesh['rows_0'=4,'rows_1'=4,'rows_2'=4,'rows_3'=2] {'rows_3'}, use_global_device_ids=true, to_apply=%region_10.11 | all-reduce | flops 2 | bytes 16 | tf_op jit(solution)/shard_map/psum | solution.py:22
  142.3 0.6 pad_maximum_fusion.4
  (158 shorter events, 10.5 us)
Async XLA Ops:
  0.6 16.1 %copy-start = (f32[16,4096]{1,0:T(8,128)S(1)}, f32[16,4096]{1,0:T(8,128)}, u32[]{:S(2)}) copy-start(f32[16,4096]{1,0:T(8,128)} %param.6) | copy-start | bytes 786436
  0.6 13.9 %copy-start.1 = (f32[16,4096]{1,0:T(8,128)S(1)}, f32[16,4096]{1,0:T(8,128)}, u32[]{:S(2)}) copy-start(f32[16,4096]{1,0:T(8,128)} %param.5) | copy-start | bytes 786436
  29.9 6.5 %collective-permute-start = (f32[3,4096]{1,0:T(4,128)S(1)}, f32[3,4096]{1,0:T(4,128)S(1)}, u32[]{:S(2)}, u32[]{:S(2)}) collective-permute-start(f32[3,4096]{1,0:T(4,128)S(1)} %pad_maximum_fusion.2), channel_id=1, source_target_pairs={{1,0},{2,1},{3,2},{4,3},{5,4},{6,5},{7,6},{8,7},{9,8},{10,9},{11,1... | collective-permute-start | bytes 147464 | tf_op jit(solution)/shard_map/ppermute | solution.py:17
  89.4 18.6 %copy-start.2 = (f32[16,4096]{1,0:T(8,128)S(1)}, f32[16,4096]{1,0:T(8,128)}, u32[]{:S(2)}) copy-start(f32[16,4096]{1,0:T(8,128)} %param.7) | copy-start | bytes 786436
where the time goes:
time: 143 us
  blocking collectives  69.5 us (49%)
  other arithmetic  34.5 us (24%)
  local copies, waits for them, and re-layouts  15.4 us (11%)
  matrix products  12.6 us (9%)
  between operations  4.34 us (3%)
  starting transfers between devices  3.29 us (2%)
  waiting for transfers between devices  3.23 us (2%)
    psum x4, blocking collectives, over_axes(): x = lax.psum(x, axis)  31.7 us
    all_to_all x1, blocking collectives, body(): lax.all_to_all(tip_rows, ROWS, split_axis=2, concat_axis=0, tiled=True)  23.4 us
    unnamed x1, other arithmetic  19.6 us
    all_to_all x1, blocking collectives, body(): lax.all_to_all(paired, ROWS, split_axis=0, concat_axis=2, tiled=True)  14.5 us
    dot_general x1, matrix products, body(): jnp.dot(weights, history.reshape(level_count, local_rows * width_cells),...  12.6 us
    unnamed x9, local copies, waits for them, and re-layouts  7.31 us
    sub x19, other arithmetic, cyclic_solve(): operand - factor_up * take_from(operand, stride, 0.0, along, True)  5.36 us
    slice x51, local copies, waits for them, and re-layouts, take_from(): kept = lax.slice_in_dim(array_in, 0, length - stride, 1, along)  3.46 us
  transfers between devices with their start and end apart: 1, of which 1 were waited for; matrix products, arithmetic and copies ran while one was open for 0% of the time, Pallas kernels for 0%

commit v1 on v0

v1 whole, which is shorter than its diff:
```python
import jax
import jax.numpy as jnp
import numpy as np
from jax import lax
from jax.experimental import pallas as pl
from jax.experimental.pallas import tpu as pltpu
from jax.sharding import PartitionSpec as P

STIFF = 1024.0
ORDER = 0.6
AXIS = "rows"
LANES = 128
SUB = 8
LEVELS = 32
ROWS = 16
NY = 4096
TILES = NY // LANES
HALVES = ROWS // SUB
VREGS = HALVES * TILES
BLOCKS = 128
INNER = ROWS - 1
CHUNKS = 8
CHUNK_TILES = TILES // CHUNKS
STEPS = 12
F32 = jnp.float32


def history_weights():
    moments = np.arange(LEVELS + 1, dtype=np.float64) ** (1.0 - ORDER)
    b = moments[1:] - moments[:-1]
    w = np.concatenate([b[1:], [0.0]]) - np.concatenate([[0.0], b[1:]])
    scale = -w
    scale[0] = 1.0 - w[0]
    return [float(v) for v in scale.astype(np.float32)]


def tile(h, t):
    return pl.ds((h * TILES + t % TILES) * SUB, SUB)


def line(r):
    return pl.ds((r // SUB) * TILES * SUB + r % SUB, TILES, stride=SUB)


def wide(r):
    return pl.ds(r * TILES, TILES)


def shifted(values, stride, lane):
    if stride >= LANES:
        hop = stride // LANES
        low = [values[(t - hop) % TILES] for t in range(TILES)]
        high = [values[(t + hop) % TILES] for t in range(TILES)]
        return low, high
    down = [pltpu.roll(v, stride, 1) for v in values]
    up = [pltpu.roll(v, LANES - stride, 1) for v in values]
    low = [jnp.where(lane < stride, down[t - 1], down[t]) for t in range(TILES)]
    high = [
        jnp.where(lane >= LANES - stride, up[(t + 1) % TILES], up[t]) for t in range(TILES)
    ]
    return low, high


def local_kernel(
    hist_hbm, src_hbm, dif_hbm, tgt_hbm,
    msg, part, above, below,
    hist, src, dif, tgt,
    alpha, beta, main, sub, sup, inv, rhs,
    dif_l, tgt_l, sw_l, gg, hh, rr, pp,
    sems,
):
    copies = [
        pltpu.make_async_copy(dif_hbm, dif, sems.at[0]),
        pltpu.make_async_copy(src_hbm, src, sems.at[1]),
    ]
    width = CHUNK_TILES * LANES
    for c in range(CHUNKS):
        cols = pl.ds(c * width, width)
        copies.append(
            pltpu.make_async_copy(
                hist_hbm.at[:, :, cols], hist.at[:, :, cols], sems.at[3 + c]
            )
        )
    copies.append(pltpu.make_async_copy(tgt_hbm, tgt, sems.at[2]))
    for copy in copies:
        copy.start()
    lane = lax.broadcasted_iota(jnp.int32, (SUB, LANES), 1)

    copies[0].wait()
    for h in range(HALVES):
        for t in range(TILES):
            c = STIFF * dif[h * SUB:(h + 1) * SUB, t * LANES:(t + 1) * LANES]
            dif_l[tile(h, t), :] = c
            m = 1.0 + 2.0 * c
            main[0, tile(h, t), :] = m
            inv[0, tile(h, t), :] = 1.0 / m
            sub[0, tile(h, t), :] = jnp.where(lane == 0, 0.0, c) if t == 0 else c
            sup[0, tile(h, t), :] = jnp.where(lane == LANES - 1, 0.0, c) if t == TILES - 1 else c

    g = h_ = None
    for r in range(ROWS):
        c = dif_l[line(r), :]
        if r == 0:
            q = 1.0 / (1.0 + 2.0 * c)
            g = c * q
            h_ = g
        else:
            q = 1.0 / (1.0 + 2.0 * c - c * g)
            g = c * q
            h_ = g * h_
        rr[wide(r), :] = q
        gg[wide(r), :] = g
        hh[wide(r), :] = h_
    a = hh[wide(INNER - 1), :]
    b = gg[wide(INNER - 1), :]
    zero = jnp.zeros((TILES, LANES), F32)
    sum_a = sum_b = sum_aa = sum_ab = sum_bb = zero
    for r in reversed(range(INNER)):
        if r < INNER - 1:
            g = gg[wide(r), :]
            a = hh[wide(r), :] + g * a
            b = g * b
        above[wide(r), :] = a
        below[wide(r), :] = b
        sum_a = sum_a + a
        sum_b = sum_b + b
        sum_aa = sum_aa + a * a
        sum_ab = sum_ab + a * b
        sum_bb = sum_bb + b * b
    def send(group, four):
        stacked = jnp.concatenate(four, axis=0)
        msg[pl.ds(group, BLOCKS, stride=4), :] = stacked.T

    send(0, [a, b, hh[wide(INNER), :], gg[wide(INNER), :]])
    send(1, [sum_a, sum_b + 1.0, sum_aa, sum_ab])

    for k in range(STEPS):
        stride = 1 << k
        now = k % 2
        nxt = 1 - now
        for h in range(HALVES):
            e = [sub[now, tile(h, t), :] for t in range(TILES)]
            f = [sup[now, tile(h, t), :] for t in range(TILES)]
            v = [inv[now, tile(h, t), :] for t in range(TILES)]
            e_low, e_high = shifted(e, stride, lane)
            f_low, f_high = shifted(f, stride, lane)
            v_low, v_high = shifted(v, stride, lane)
            for t in range(TILES):
                al = e[t] * v_low[t]
                be = f[t] * v_high[t]
                m = main[now, tile(h, t), :] - al * f_low[t] - be * e_high[t]
                alpha[k, tile(h, t), :] = al
                beta[k, tile(h, t), :] = be
                if k < STEPS - 1:
                    main[nxt, tile(h, t), :] = m
                    sub[nxt, tile(h, t), :] = al * e_low[t]
                    sup[nxt, tile(h, t), :] = be * f_high[t]
                inv[nxt, tile(h, t), :] = 1.0 / m

    scale = history_weights()
    copies[1].wait()
    for c in range(CHUNKS):
        copies[2 + c].wait()
        for h in range(HALVES):
            rows = slice(h * SUB, (h + 1) * SUB)
            for t in range(c * CHUNK_TILES, (c + 1) * CHUNK_TILES):
                cols = slice(t * LANES, (t + 1) * LANES)
                acc = src[rows, cols]
                for k in range(LEVELS):
                    acc = acc + scale[k] * hist[k, rows, cols]
                rhs[0, tile(h, t), :] = acc

    for k in range(STEPS):
        now = k % 2
        nxt = 1 - now
        for h in range(HALVES):
            d = [rhs[now, tile(h, t), :] for t in range(TILES)]
            low, high = shifted(d, 1 << k, lane)
            for t in range(TILES):
                n = (
                    d[t]
                    + alpha[k, tile(h, t), :] * low[t]
                    + beta[k, tile(h, t), :] * high[t]
                )
                if k < STEPS - 1:
                    rhs[nxt, tile(h, t), :] = n
                else:
                    sw_l[tile(h, t), :] = n * inv[nxt, tile(h, t), :]

    copies[2 + CHUNKS].wait()
    for h in range(HALVES):
        for t in range(TILES):
            tgt_l[tile(h, t), :] = tgt[h * SUB:(h + 1) * SUB, t * LANES:(t + 1) * LANES]
    p = None
    for r in range(ROWS):
        s = rr[wide(r), :] * sw_l[line(r), :]
        p = s if r == 0 else s + gg[wide(r), :] * p
        pp[wide(r), :] = p
    tip = p
    d = tgt_l[line(INNER), :]
    sum_dd = d * d
    sum_db = -d
    sum_da = zero
    sum_p = zero
    p = pp[wide(INNER - 1), :]
    for r in reversed(range(INNER)):
        if r < INNER - 1:
            p = pp[wide(r), :] + gg[wide(r), :] * p
        part[wide(r), :] = p
        a = above[wide(r), :]
        b = below[wide(r), :]
        d = p - tgt_l[line(r), :]
        sum_p = sum_p + p
        sum_dd = sum_dd + d * d
        sum_da = sum_da + d * a
        sum_db = sum_db + d * b
    send(2, [p, tip, sum_p, sum_dd])
    send(3, [sum_da, sum_db, sum_bb + 1.0, zero])


def reduced_kernel(got, back):
    groups = [got[pl.ds(g, BLOCKS, stride=4), :].T for g in range(4)]
    q = [groups[i // 4][(i % 4) * TILES:(i % 4 + 1) * TILES] for i in range(15)]
    (a0, b0, u, v, sum_a, sum_b, sum_aa, sum_ab, p0, w, sum_p, sum_dd, sum_da, sum_db, sum_bb) = q
    lane = lax.broadcasted_iota(jnp.int32, (TILES, LANES), 1)
    u = jnp.where(lane == 0, 0.0, u)
    v = jnp.where(lane == BLOCKS - 1, 0.0, v)

    def low(x, s):
        return pltpu.roll(x, s, 1)

    def high(x, s):
        return pltpu.roll(x, LANES - s, 1)

    r = 1.0 / (1.0 - v * high(a0, 1))
    e = u * r
    f = v * high(b0, 1) * r
    d = (w + v * high(p0, 1)) * r
    s = 1
    while s < BLOCKS:
        r = 1.0 / (1.0 - e * low(f, s) - f * high(e, s))
        d = (d + e * low(d, s) + f * high(d, s)) * r
        if 2 * s < BLOCKS:
            e, f = e * low(e, s) * r, f * high(f, s) * r
        s *= 2
    z = d
    x = jnp.where(lane == 0, 0.0, low(z, 1))
    mass = sum_p + sum_a * x + sum_b * z
    error = (
        sum_dd
        + 2.0 * (sum_da * x + sum_db * z + sum_ab * x * z)
        + sum_aa * x * x
        + sum_bb * z * z
    )

    def total(y):
        y = jnp.sum(jnp.sum(y, axis=0, keepdims=True), axis=1, keepdims=True)
        return jnp.broadcast_to(y, (SUB, LANES))

    rest = jnp.zeros((LANES - 2 * TILES - 2 * SUB, LANES), F32)
    back[...] = jnp.concatenate([z, x, total(mass), total(error), rest], axis=0).T


def final_kernel(got, part, above, below, update, totals, lines):
    t = got[...].T
    z = t[:TILES]
    x = t[TILES:2 * TILES]
    scale = 1.0 / (BLOCKS * ROWS * NY)
    totals[0] = jnp.sum(t[2 * TILES:2 * TILES + 1]) * scale
    totals[1] = jnp.sum(t[2 * TILES + SUB:2 * TILES + SUB + 1]) * scale
    for r in range(INNER):
        lines[line(r), :] = part[wide(r), :] + above[wide(r), :] * x + below[wide(r), :] * z
    lines[line(INNER), :] = z
    for h in range(HALVES):
        for i in range(TILES):
            update[h * SUB:(h + 1) * SUB, i * LANES:(i + 1) * LANES] = lines[tile(h, i), :]


def body(history, source, diffusivity, target):
    anywhere = pl.BlockSpec(memory_space=pl.ANY)
    vmem = pl.BlockSpec(memory_space=pltpu.VMEM)
    shape = jax.ShapeDtypeStruct
    block = pltpu.VMEM((ROWS, NY), F32)
    tiles = pltpu.VMEM((VREGS * SUB, LANES), F32)
    pair = pltpu.VMEM((2, VREGS * SUB, LANES), F32)
    lines = INNER * TILES
    params = pltpu.CompilerParams(vmem_limit_bytes=48 * 1024 * 1024)
    msg, part, above, below = pl.pallas_call(
        local_kernel,
        name="local",
        out_shape=[shape((4 * BLOCKS, LANES), F32)] + [shape((lines, LANES), F32)] * 3,
        in_specs=[anywhere] * 4,
        out_specs=[vmem] * 4,
        scratch_shapes=[
            pltpu.VMEM((LEVELS, ROWS, NY), F32), block, block, block,
            pltpu.VMEM((STEPS, VREGS * SUB, LANES), F32),
            pltpu.VMEM((STEPS, VREGS * SUB, LANES), F32),
            pair, pair, pair, pair, pair,
            tiles, tiles, tiles, tiles, tiles, tiles, tiles,
            pltpu.SemaphoreType.DMA((3 + CHUNKS,)),
        ],
        compiler_params=params,
    )(history, source, diffusivity, target)
    got = lax.all_to_all(
        msg.reshape(BLOCKS, 4, LANES), AXIS, split_axis=0, concat_axis=0, tiled=True
    ).reshape(4 * BLOCKS, LANES)
    back = pl.pallas_call(
        reduced_kernel,
        name="reduced",
        out_shape=shape((BLOCKS, LANES), F32),
        in_specs=[vmem],
        out_specs=vmem,
        compiler_params=params,
    )(got)
    solved = lax.all_to_all(back, AXIS, split_axis=0, concat_axis=0, tiled=True)
    return pl.pallas_call(
        final_kernel,
        name="final",
        out_shape=[shape((ROWS, NY), F32), shape((2,), F32)],
        in_specs=[vmem] * 4,
        out_specs=[vmem, pl.BlockSpec(memory_space=pltpu.SMEM)],
        scratch_shapes=[tiles],
        compiler_params=params,
    )(solved, part, above, below)


def solution(mesh):
    return jax.shard_map(
        body,
        mesh=mesh,
        in_specs=(P(None, AXIS, None), P(AXIS, None), P(AXIS, None), P(AXIS, None)),
        out_specs=(P(AXIS, None), P()),
        check_vma=False,
    )
```

time: 143 us -> 47.5 us (0.33)
  other arithmetic: 34.5 us -> 0 us
  blocking collectives: 69.5 us -> 36.1 us
  matrix products: 12.6 us -> 0 us
  local copies, waits for them, and re-layouts: 15.4 us -> 2.84 us
  Pallas kernels: 0 us -> 7.66 us
  between operations: 4.34 us -> 0.66 us
  starting transfers between devices: 3.29 us -> 0 us
  waiting for transfers between devices: 3.23 us -> 0 us
    psum x4 -> x0, blocking collectives: 31.7 us -> none  [over_axes(): x = lax.psum(x, axis)]
    unnamed x1 -> x0, other arithmetic: 19.6 us -> none
    dot_general x1 -> x0, matrix products: 12.6 us -> none  [body(): jnp.dot(weights, history.reshape(level_count, local_rows * width_cells),...]
    sub x38 -> x0, other arithmetic: 7.94 us -> none  [the longest x19 5.36 us: cyclic_solve(): operand - factor_up * take_from(operand, stride, 0.0, along, True)]
    pallas_call x0 -> x3, Pallas kernels: none -> 7.66 us  [the longest x1 5.74 us: body(): pl.pallas_call(local_kernel, name='local', out_shape=[shape((4 * BLOCKS,...]
    slice x101 -> x0, local copies, waits for them, and re-layouts: 6.08 us -> none  [the longest x51 3.46 us: take_from(): kept = lax.slice_in_dim(array_in, 0, length - stride, 1, along)]
    unnamed x9 -> x6, local copies, waits for them, and re-layouts: 7.31 us -> 2.84 us
    ppermute x1 -> x0, starting transfers between devices: 3.29 us -> none  [shifted(): lax.ppermute(value, axis, [(source, source + steps) for source in range(l...]
  transfers between devices with their start and end apart: 1 -> 0, of which waited for: 1 -> 0; matrix products, arithmetic and copies ran while one was open for 0% -> 0% of each run, Pallas kernels for 0% -> 0%
where the time goes in v1:
time: 47.5 us; the launch traced here: 47.3 us
  blocking collectives  36.1 us (76%)
  Pallas kernels  7.66 us (16%)
  local copies, waits for them, and re-layouts  2.84 us (6%)
  between operations  0.66 us (1%)
    all_to_all x1, blocking collectives, body(): lax.all_to_all(msg.reshape(BLOCKS, 4, LANES), AXIS, split_axis=0, concat_...  22.2 us
    all_to_all x1, blocking collectives, body(): solved = lax.all_to_all(back, AXIS, split_axis=0, concat_axis=0, tiled=True)  14 us
    pallas_call x1, Pallas kernels, body(): pl.pallas_call(local_kernel, name='local', out_shape=[shape((4 * BLOCKS,...  5.74 us
    unnamed x6, local copies, waits for them, and re-layouts  2.84 us
    pallas_call x1, Pallas kernels, body(): pl.pallas_call(reduced_kernel, name='reduced', out_shape=shape((BLOCKS, L...  1.06 us

profile of v1, /device:TPU:1, one launch (start us, length us, event | category | flops | bytes accessed | tf_op | source)
XLA Modules:
  0.0 47.3 jit_solution(3278567089170691345)
XLA Ops:
  0.6 0.0 copy-start
  0.6 0.9 %copy-done = f32[16,4096]{1,0:T(8,128)S(1)} copy-done((f32[16,4096]{1,0:T(8,128)S(1)}, f32[16,4096]{1,0:T(8,128)}, u32[]{:S(2)}) %copy-start) | copy-done | bytes 262168
  1.6 0.0 copy-start.1
  1.6 0.9 %copy-done.1 = f32[16,4096]{1,0:T(8,128)S(1)} copy-done((f32[16,4096]{1,0:T(8,128)S(1)}, f32[16,4096]{1,0:T(8,128)}, u32[]{:S(2)}) %copy-start.1) | copy-done | bytes 262168
  2.5 0.0 copy-start.2
  2.5 0.9 %copy-done.2 = f32[16,4096]{1,0:T(8,128)S(1)} copy-done((f32[16,4096]{1,0:T(8,128)S(1)}, f32[16,4096]{1,0:T(8,128)}, u32[]{:S(2)}) %copy-start.2) | copy-done | bytes 262168
  3.5 5.7 %local.1 = (f32[512,128]{1,0:T(8,128)S(1)}, f32[480,128]{1,0:T(8,128)S(1)}, f32[480,128]{1,0:T(8,128)S(1)}, f32[480,128]{1,0:T(8,128)S(1)}) custom-call(f32[32,16,4096]{2,1,0:T(8,128)} %hist_hbm.1, f32[16,4096]{1,0:T(8,128)S(1)} %copy-done, f32[16,4096]{1,0:T(8,128)S(1)} %copy-done.1, f32[16,4096]{1,0:T(8,128)S(1)} %copy-done.2), custom_call_target="tpu_custom_call" | custom-call | tf_op jit(solution)/shard_map/local/pallas_call | solution.py:288
  9.2 22.2 %all_to_all.16 = f32[128,4,128]{2,1,0:T(4,128)S(1)} all-to-all(f32[128,4,128]{2,1,0:T(4,128)S(1)} %bitcast.9), channel_id=1, replica_groups=mesh['rows'=128] {'rows'}, dimensions={0} | all-to-all | bytes 524288 | tf_op jit(solution)/shard_map/all_to_all | solution.py:304
  31.4 1.1 %reduced.1 = f32[128,128]{1,0:T(8,128)S(1)} custom-call(f32[512,128]{1,0:T(8,128)S(1)} %bitcast.6), custom_call_target="tpu_custom_call" | custom-call | tf_op jit(solution)/shard_map/reduced/pallas_call | solution.py:307
  32.5 14.0 %all_to_all.17 = f32[128,1,128]{2,1,0:T(1,128)S(1)} all-to-all(f32[128,1,128]{2,1,0:T(1,128)S(1)} %bitcast.8), channel_id=1, replica_groups=mesh['rows'=128] {'rows'}, dimensions={0} | all-to-all | bytes 131072 | tf_op jit(solution)/shard_map/all_to_all | solution.py:315
  46.4 0.9 %final.1 = (f32[16,4096]{1,0:T(8,128)}, f32[2]{0:T(128)}) custom-call(f32[128,128]{1,0:T(8,128)S(1)} %bitcast.7, f32[480,128]{1,0:T(8,128)S(1)} %get-tuple-element.7.part, f32[480,128]{1,0:T(8,128)S(1)} %get-tuple-element.8.above, f32[480,128]{1,0:T(8,128)S(1)} %get-tuple-element.9.below), custom_call_target="tpu_custom_call" | custom-call | tf_op jit(solution)/shard_map/final/pallas_call | solution.py:316
Async XLA Ops:
  0.6 1.0 %copy-start = (f32[16,4096]{1,0:T(8,128)S(1)}, f32[16,4096]{1,0:T(8,128)}, u32[]{:S(2)}) copy-start(f32[16,4096]{1,0:T(8,128)} %src_hbm.1) | copy-start | bytes 786436
  1.6 0.9 %copy-start.1 = (f32[16,4096]{1,0:T(8,128)S(1)}, f32[16,4096]{1,0:T(8,128)}, u32[]{:S(2)}) copy-start(f32[16,4096]{1,0:T(8,128)} %dif_hbm.1) | copy-start | bytes 786436
  2.5 0.9 %copy-start.2 = (f32[16,4096]{1,0:T(8,128)S(1)}, f32[16,4096]{1,0:T(8,128)}, u32[]{:S(2)}) copy-start(f32[16,4096]{1,0:T(8,128)} %tgt_hbm.1) | copy-start | bytes 786436

commit v2 on v1

--- a/solution.py
+++ b/solution.py
@@ -277,7 +277,7 @@
 
 
 def body(history, source, diffusivity, target):
-    anywhere = pl.BlockSpec(memory_space=pl.ANY)
+    anywhere = pl.BlockSpec(memory_space=pltpu.HBM)
     vmem = pl.BlockSpec(memory_space=pltpu.VMEM)
     shape = jax.ShapeDtypeStruct
     block = pltpu.VMEM((ROWS, NY), F32)
@@ -300,7 +300,7 @@
             pltpu.SemaphoreType.DMA((3 + CHUNKS,)),
         ],
         compiler_params=params,
-    )(history, source, diffusivity, target)
+    )(*(pltpu.with_memory_space_constraint(x, pltpu.HBM) for x in (history, source, diffusivity, target)))
     got = lax.all_to_all(
         msg.reshape(BLOCKS, 4, LANES), AXIS, split_axis=0, concat_axis=0, tiled=True
     ).reshape(4 * BLOCKS, LANES)

time: 47.5 us -> 45.5 us (0.958)
  local copies, waits for them, and re-layouts: 2.84 us -> 0 us
  Pallas kernels: 7.66 us -> 8.55 us
    unnamed x6 -> x0, local copies, waits for them, and re-layouts: 2.84 us -> none
    pallas_call x1, Pallas kernels: 5.74 us -> 6.62 us  [body(): pl.pallas_call(local_kernel, name='local', out_shape=[shape((4 * BLOCKS,...]
where the time goes in v2:
time: 45.5 us; the launch traced here: 45.3 us
  blocking collectives  36.1 us (79%)
  Pallas kernels  8.55 us (19%)
  between operations  0.65 us (1%)
    all_to_all x1, blocking collectives, body(): lax.all_to_all(msg.reshape(BLOCKS, 4, LANES), AXIS, split_axis=0, concat_...  22.2 us
    all_to_all x1, blocking collectives, body(): solved = lax.all_to_all(back, AXIS, split_axis=0, concat_axis=0, tiled=True)  14 us
    pallas_call x1, Pallas kernels, body(): pl.pallas_call(local_kernel, name='local', out_shape=[shape((4 * BLOCKS,...  6.62 us
    pallas_call x1, Pallas kernels, body(): pl.pallas_call(reduced_kernel, name='reduced', out_shape=shape((BLOCKS, L...  1.06 us

profile of v2, /device:TPU:1, one launch (start us, length us, event | category | flops | bytes accessed | tf_op | source)
XLA Modules:
  0.0 45.3 jit_solution(16112173454372885335)
XLA Ops:
  0.6 6.6 %local.1 = (f32[512,128]{1,0:T(8,128)S(1)}, f32[480,128]{1,0:T(8,128)S(1)}, f32[480,128]{1,0:T(8,128)S(1)}, f32[480,128]{1,0:T(8,128)S(1)}) custom-call(f32[32,16,4096]{2,1,0:T(8,128)} %hist_hbm.1, f32[16,4096]{1,0:T(8,128)} %src_hbm.1, f32[16,4096]{1,0:T(8,128)} %dif_hbm.1, f32[16,4096]{1,0:T(8,128)} %tgt_hbm.1), custom_call_target="tpu_custom_call" | custom-call | tf_op jit(solution)/shard_map/local/pallas_call | solution.py:288
  7.3 22.2 %all_to_all.16 = f32[128,4,128]{2,1,0:T(4,128)S(1)} all-to-all(f32[128,4,128]{2,1,0:T(4,128)S(1)} %bitcast.9), channel_id=1, replica_groups=mesh['rows'=128] {'rows'}, dimensions={0} | all-to-all | bytes 524288 | tf_op jit(solution)/shard_map/all_to_all | solution.py:304
  29.4 1.1 %reduced.1 = f32[128,128]{1,0:T(8,128)S(1)} custom-call(f32[512,128]{1,0:T(8,128)S(1)} %bitcast.6), custom_call_target="tpu_custom_call" | custom-call | tf_op jit(solution)/shard_map/reduced/pallas_call | solution.py:307
  30.5 14.0 %all_to_all.17 = f32[128,1,128]{2,1,0:T(1,128)S(1)} all-to-all(f32[128,1,128]{2,1,0:T(1,128)S(1)} %bitcast.8), channel_id=1, replica_groups=mesh['rows'=128] {'rows'}, dimensions={0} | all-to-all | bytes 131072 | tf_op jit(solution)/shard_map/all_to_all | solution.py:315
  44.5 0.9 %final.1 = (f32[16,4096]{1,0:T(8,128)}, f32[2]{0:T(128)}) custom-call(f32[128,128]{1,0:T(8,128)S(1)} %bitcast.7, f32[480,128]{1,0:T(8,128)S(1)} %get-tuple-element.7.part, f32[480,128]{1,0:T(8,128)S(1)} %get-tuple-element.8.above, f32[480,128]{1,0:T(8,128)S(1)} %get-tuple-element.9.below), custom_call_target="tpu_custom_call" | custom-call | tf_op jit(solution)/shard_map/final/pallas_call | solution.py:316

commit v3 on v2

--- a/solution.py
+++ b/solution.py
@@ -19,7 +19,7 @@
 VREGS = HALVES * TILES
 BLOCKS = 128
 INNER = ROWS - 1
-CHUNKS = 8
+CHUNKS = 4
 CHUNK_TILES = TILES // CHUNKS
 STEPS = 12
 F32 = jnp.float32
@@ -46,42 +46,47 @@
     return pl.ds(r * TILES, TILES)
 
 
-def shifted(values, stride, lane):
+def neighbours(load, stride, lane):
     if stride >= LANES:
         hop = stride // LANES
-        low = [values[(t - hop) % TILES] for t in range(TILES)]
-        high = [values[(t + hop) % TILES] for t in range(TILES)]
-        return low, high
-    down = [pltpu.roll(v, stride, 1) for v in values]
-    up = [pltpu.roll(v, LANES - stride, 1) for v in values]
-    low = [jnp.where(lane < stride, down[t - 1], down[t]) for t in range(TILES)]
-    high = [
-        jnp.where(lane >= LANES - stride, up[(t + 1) % TILES], up[t]) for t in range(TILES)
-    ]
-    return low, high
+        for t in range(TILES):
+            yield load(t), load(t - hop), load(t + hop)
+        return
+    back = LANES - stride
+    before = pltpu.roll(load(TILES - 1), stride, 1)
+    first = pltpu.roll(load(0), back, 1)
+    here = first
+    for t in range(TILES):
+        value = load(t)
+        down = pltpu.roll(value, stride, 1)
+        after = first if t == TILES - 1 else pltpu.roll(load(t + 1), back, 1)
+        yield value, jnp.where(lane < stride, before, down), jnp.where(lane >= back, after, here)
+        before, here = down, after
 
 
 def local_kernel(
     hist_hbm, src_hbm, dif_hbm, tgt_hbm,
     msg, part, above, below,
     hist, src, dif, tgt,
-    alpha, beta, main, sub, sup, inv, rhs,
+    lower, upper, pivot, first, rhs,
     dif_l, tgt_l, sw_l, gg, hh, rr, pp,
     sems,
 ):
     copies = [
         pltpu.make_async_copy(dif_hbm, dif, sems.at[0]),
         pltpu.make_async_copy(src_hbm, src, sems.at[1]),
+        pltpu.make_async_copy(tgt_hbm, tgt, sems.at[2]),
     ]
     width = CHUNK_TILES * LANES
-    for c in range(CHUNKS):
-        cols = pl.ds(c * width, width)
-        copies.append(
-            pltpu.make_async_copy(
-                hist_hbm.at[:, :, cols], hist.at[:, :, cols], sems.at[3 + c]
+    for h in range(HALVES):
+        rows = pl.ds(h * SUB, SUB)
+        for c in range(CHUNKS):
+            cols = pl.ds(c * width, width)
+            copies.append(
+                pltpu.make_async_copy(
+                    hist_hbm.at[:, rows, cols], hist.at[:, rows, cols], sems.at[len(copies)]
+                )
             )
-        )
-    copies.append(pltpu.make_async_copy(tgt_hbm, tgt, sems.at[2]))
     for copy in copies:
         copy.start()
     lane = lax.broadcasted_iota(jnp.int32, (SUB, LANES), 1)
@@ -91,11 +96,11 @@
         for t in range(TILES):
             c = STIFF * dif[h * SUB:(h + 1) * SUB, t * LANES:(t + 1) * LANES]
             dif_l[tile(h, t), :] = c
-            m = 1.0 + 2.0 * c
-            main[0, tile(h, t), :] = m
-            inv[0, tile(h, t), :] = 1.0 / m
-            sub[0, tile(h, t), :] = jnp.where(lane == 0, 0.0, c) if t == 0 else c
-            sup[0, tile(h, t), :] = jnp.where(lane == LANES - 1, 0.0, c) if t == TILES - 1 else c
+            q = 1.0 / (1.0 + 2.0 * c)
+            first[tile(h, t), :] = q
+            c = c * q
+            lower[0, tile(h, t), :] = jnp.where(lane == 0, 0.0, c) if t == 0 else c
+            upper[0, tile(h, t), :] = jnp.where(lane == LANES - 1, 0.0, c) if t == TILES - 1 else c
 
     g = h_ = None
     for r in range(ROWS):
@@ -135,62 +140,48 @@
     send(1, [sum_a, sum_b + 1.0, sum_aa, sum_ab])
 
     for k in range(STEPS):
-        stride = 1 << k
-        now = k % 2
-        nxt = 1 - now
         for h in range(HALVES):
-            e = [sub[now, tile(h, t), :] for t in range(TILES)]
-            f = [sup[now, tile(h, t), :] for t in range(TILES)]
-            v = [inv[now, tile(h, t), :] for t in range(TILES)]
-            e_low, e_high = shifted(e, stride, lane)
-            f_low, f_high = shifted(f, stride, lane)
-            v_low, v_high = shifted(v, stride, lane)
+            lows = neighbours(lambda t: lower[k, tile(h, t), :], 1 << k, lane)
+            highs = neighbours(lambda t: upper[k, tile(h, t), :], 1 << k, lane)
             for t in range(TILES):
-                al = e[t] * v_low[t]
-                be = f[t] * v_high[t]
-                m = main[now, tile(h, t), :] - al * f_low[t] - be * e_high[t]
-                alpha[k, tile(h, t), :] = al
-                beta[k, tile(h, t), :] = be
+                e, e_low, e_high = next(lows)
+                f, f_low, f_high = next(highs)
+                q = 1.0 / (1.0 - e * f_low - f * e_high)
+                pivot[k, tile(h, t), :] = q
                 if k < STEPS - 1:
-                    main[nxt, tile(h, t), :] = m
-                    sub[nxt, tile(h, t), :] = al * e_low[t]
-                    sup[nxt, tile(h, t), :] = be * f_high[t]
-                inv[nxt, tile(h, t), :] = 1.0 / m
+                    lower[k + 1, tile(h, t), :] = e * e_low * q
+                    upper[k + 1, tile(h, t), :] = f * f_high * q
 
     scale = history_weights()
     copies[1].wait()
-    for c in range(CHUNKS):
-        copies[2 + c].wait()
-        for h in range(HALVES):
-            rows = slice(h * SUB, (h + 1) * SUB)
+    copies[2].wait()
+    for h in range(HALVES):
+        rows = slice(h * SUB, (h + 1) * SUB)
+        for t in range(TILES):
+            tgt_l[tile(h, t), :] = tgt[rows, t * LANES:(t + 1) * LANES]
+    for h in range(HALVES):
+        rows = slice(h * SUB, (h + 1) * SUB)
+        for c in range(CHUNKS):
+            copies[3 + h * CHUNKS + c].wait()
             for t in range(c * CHUNK_TILES, (c + 1) * CHUNK_TILES):
                 cols = slice(t * LANES, (t + 1) * LANES)
                 acc = src[rows, cols]
                 for k in range(LEVELS):
                     acc = acc + scale[k] * hist[k, rows, cols]
-                rhs[0, tile(h, t), :] = acc
-
-    for k in range(STEPS):
-        now = k % 2
-        nxt = 1 - now
-        for h in range(HALVES):
-            d = [rhs[now, tile(h, t), :] for t in range(TILES)]
-            low, high = shifted(d, 1 << k, lane)
+                rhs[0, tile(h, t), :] = acc * first[tile(h, t), :]
+        for k in range(STEPS):
+            now = k % 2
+            values = neighbours(lambda t: rhs[now, tile(h, t), :], 1 << k, lane)
             for t in range(TILES):
-                n = (
-                    d[t]
-                    + alpha[k, tile(h, t), :] * low[t]
-                    + beta[k, tile(h, t), :] * high[t]
-                )
+                d, low, high = next(values)
+                d = (
+                    d + lower[k, tile(h, t), :] * low + upper[k, tile(h, t), :] * high
+                ) * pivot[k, tile(h, t), :]
                 if k < STEPS - 1:
-                    rhs[nxt, tile(h, t), :] = n
+                    rhs[1 - now, tile(h, t), :] = d
                 else:
-                    sw_l[tile(h, t), :] = n * inv[nxt, tile(h, t), :]
-
-    copies[2 + CHUNKS].wait()
-    for h in range(HALVES):
-        for t in range(TILES):
-            tgt_l[tile(h, t), :] = tgt[h * SUB:(h + 1) * SUB, t * LANES:(t + 1) * LANES]
+                    sw_l[tile(h, t), :] = d
+
     p = None
     for r in range(ROWS):
         s = rr[wide(r), :] * sw_l[line(r), :]
@@ -283,6 +274,7 @@
     block = pltpu.VMEM((ROWS, NY), F32)
     tiles = pltpu.VMEM((VREGS * SUB, LANES), F32)
     pair = pltpu.VMEM((2, VREGS * SUB, LANES), F32)
+    stages = pltpu.VMEM((STEPS, VREGS * SUB, LANES), F32)
     lines = INNER * TILES
     params = pltpu.CompilerParams(vmem_limit_bytes=48 * 1024 * 1024)
     msg, part, above, below = pl.pallas_call(
@@ -293,11 +285,9 @@
         out_specs=[vmem] * 4,
         scratch_shapes=[
             pltpu.VMEM((LEVELS, ROWS, NY), F32), block, block, block,
-            pltpu.VMEM((STEPS, VREGS * SUB, LANES), F32),
-            pltpu.VMEM((STEPS, VREGS * SUB, LANES), F32),
-            pair, pair, pair, pair, pair,
+            stages, stages, stages, tiles, pair,
             tiles, tiles, tiles, tiles, tiles, tiles, tiles,
-            pltpu.SemaphoreType.DMA((3 + CHUNKS,)),
+            pltpu.SemaphoreType.DMA((3 + HALVES * CHUNKS,)),
         ],
         compiler_params=params,
     )(*(pltpu.with_memory_space_constraint(x, pltpu.HBM) for x in (history, source, diffusivity, target)))

time: 45.5 us -> 44.8 us (0.985)
  Pallas kernels: 8.55 us -> 7.88 us
    pallas_call x1, Pallas kernels: 6.62 us -> 5.95 us  [body(): pl.pallas_call(local_kernel, name='local', out_shape=[shape((4 * BLOCKS,...]
where the time goes in v3:
time: 44.8 us; the launch traced here: 44.7 us
  blocking collectives  36.1 us (81%)
  Pallas kernels  7.88 us (18%)
  between operations  0.65 us (1%)
    all_to_all x1, blocking collectives, body(): lax.all_to_all(msg.reshape(BLOCKS, 4, LANES), AXIS, split_axis=0, concat_...  22.2 us
    all_to_all x1, blocking collectives, body(): solved = lax.all_to_all(back, AXIS, split_axis=0, concat_axis=0, tiled=True)  14 us
    pallas_call x1, Pallas kernels, body(): pl.pallas_call(local_kernel, name='local', out_shape=[shape((4 * BLOCKS,...  5.95 us
    pallas_call x1, Pallas kernels, body(): pl.pallas_call(reduced_kernel, name='reduced', out_shape=shape((BLOCKS, L...  1.06 us

profile of v3, /device:TPU:1, one launch (start us, length us, event | category | flops | bytes accessed | tf_op | source)
XLA Modules:
  0.0 44.7 jit_solution(6915330294831813523)
XLA Ops:
  0.6 6.0 %local.1 = (f32[512,128]{1,0:T(8,128)S(1)}, f32[480,128]{1,0:T(8,128)S(1)}, f32[480,128]{1,0:T(8,128)S(1)}, f32[480,128]{1,0:T(8,128)S(1)}) custom-call(f32[32,16,4096]{2,1,0:T(8,128)} %hist_hbm.1, f32[16,4096]{1,0:T(8,128)} %src_hbm.1, f32[16,4096]{1,0:T(8,128)} %dif_hbm.1, f32[16,4096]{1,0:T(8,128)} %tgt_hbm.1), custom_call_target="tpu_custom_call" | custom-call | tf_op jit(solution)/shard_map/local/pallas_call | solution.py:280
  6.6 22.2 %all_to_all.16 = f32[128,4,128]{2,1,0:T(4,128)S(1)} all-to-all(f32[128,4,128]{2,1,0:T(4,128)S(1)} %bitcast.9), channel_id=1, replica_groups=mesh['rows'=128] {'rows'}, dimensions={0} | all-to-all | bytes 524288 | tf_op jit(solution)/shard_map/all_to_all | solution.py:294
  28.8 1.1 %reduced.1 = f32[128,128]{1,0:T(8,128)S(1)} custom-call(f32[512,128]{1,0:T(8,128)S(1)} %bitcast.6), custom_call_target="tpu_custom_call" | custom-call | tf_op jit(solution)/shard_map/reduced/pallas_call | solution.py:297
  29.8 14.0 %all_to_all.17 = f32[128,1,128]{2,1,0:T(1,128)S(1)} all-to-all(f32[128,1,128]{2,1,0:T(1,128)S(1)} %bitcast.8), channel_id=1, replica_groups=mesh['rows'=128] {'rows'}, dimensions={0} | all-to-all | bytes 131072 | tf_op jit(solution)/shard_map/all_to_all | solution.py:305
  43.8 0.9 %final.1 = (f32[16,4096]{1,0:T(8,128)}, f32[2]{0:T(128)}) custom-call(f32[128,128]{1,0:T(8,128)S(1)} %bitcast.7, f32[480,128]{1,0:T(8,128)S(1)} %get-tuple-element.7.part, f32[480,128]{1,0:T(8,128)S(1)} %get-tuple-element.8.above, f32[480,128]{1,0:T(8,128)S(1)} %get-tuple-element.9.below), custom_call_target="tpu_custom_call" | custom-call | tf_op jit(solution)/shard_map/final/pallas_call | solution.py:306

commit v4 on v3

--- a/solution.py
+++ b/solution.py
@@ -21,7 +21,8 @@
 INNER = ROWS - 1
 CHUNKS = 4
 CHUNK_TILES = TILES // CHUNKS
-STEPS = 12
+STEPS = 7
+MID = TILES // 2
 F32 = jnp.float32
 
 
@@ -46,37 +47,36 @@
     return pl.ds(r * TILES, TILES)
 
 
-def neighbours(load, stride, lane):
-    if stride >= LANES:
-        hop = stride // LANES
-        for t in range(TILES):
-            yield load(t), load(t - hop), load(t + hop)
-        return
+def lows(load, stride, lane):
+    before = pltpu.roll(load(TILES - 1), stride, 1)
+    for t in range(TILES):
+        down = pltpu.roll(load(t), stride, 1)
+        yield jnp.where(lane < stride, before, down)
+        before = down
+
+
+def highs(load, stride, lane):
     back = LANES - stride
-    before = pltpu.roll(load(TILES - 1), stride, 1)
-    first = pltpu.roll(load(0), back, 1)
-    here = first
+    first = here = pltpu.roll(load(0), back, 1)
     for t in range(TILES):
-        value = load(t)
-        down = pltpu.roll(value, stride, 1)
         after = first if t == TILES - 1 else pltpu.roll(load(t + 1), back, 1)
-        yield value, jnp.where(lane < stride, before, down), jnp.where(lane >= back, after, here)
-        before, here = down, after
+        yield jnp.where(lane >= back, after, here)
+        here = after
 
 
 def local_kernel(
     hist_hbm, src_hbm, dif_hbm, tgt_hbm,
     msg, part, above, below,
     hist, src, dif, tgt,
-    lower, upper, pivot, first, rhs,
+    couple, inv, main, upper, first, centre, rhs,
     dif_l, tgt_l, sw_l, gg, hh, rr, pp,
     sems,
 ):
     copies = [
         pltpu.make_async_copy(dif_hbm, dif, sems.at[0]),
         pltpu.make_async_copy(src_hbm, src, sems.at[1]),
-        pltpu.make_async_copy(tgt_hbm, tgt, sems.at[2]),
     ]
+    late = pltpu.make_async_copy(tgt_hbm, tgt, sems.at[HALVES * CHUNKS + 2])
     width = CHUNK_TILES * LANES
     for h in range(HALVES):
         rows = pl.ds(h * SUB, SUB)
@@ -87,8 +87,10 @@
                     hist_hbm.at[:, rows, cols], hist.at[:, rows, cols], sems.at[len(copies)]
                 )
             )
-    for copy in copies:
+    for i, copy in enumerate(copies):
         copy.start()
+        if i == CHUNKS + 1:
+            late.start()
     lane = lax.broadcasted_iota(jnp.int32, (SUB, LANES), 1)
 
     copies[0].wait()
@@ -96,11 +98,11 @@
         for t in range(TILES):
             c = STIFF * dif[h * SUB:(h + 1) * SUB, t * LANES:(t + 1) * LANES]
             dif_l[tile(h, t), :] = c
-            q = 1.0 / (1.0 + 2.0 * c)
+            q = 1.0 / c
             first[tile(h, t), :] = q
-            c = c * q
-            lower[0, tile(h, t), :] = jnp.where(lane == 0, 0.0, c) if t == 0 else c
-            upper[0, tile(h, t), :] = jnp.where(lane == LANES - 1, 0.0, c) if t == TILES - 1 else c
+            m = 2.0 + q
+            main[0, tile(h, t), :] = m
+            inv[0, tile(h, t), :] = 1.0 / m
 
     g = h_ = None
     for r in range(ROWS):
@@ -140,29 +142,77 @@
     send(1, [sum_a, sum_b + 1.0, sum_aa, sum_ab])
 
     for k in range(STEPS):
+        stride = 1 << k
+        now = k % 2
         for h in range(HALVES):
-            lows = neighbours(lambda t: lower[k, tile(h, t), :], 1 << k, lane)
-            highs = neighbours(lambda t: upper[k, tile(h, t), :], 1 << k, lane)
+            def v_of(t):
+                return inv[k, tile(h, t), :]
+
+            def p_of(t):
+                return v_of(t) if k == 0 else couple[k, tile(h, t), :] * v_of(t)
+
+            def s_of(t):
+                return v_of(t) if k == 0 else couple[k, tile(h, t), :] * p_of(t)
+
+            low_v = lows(v_of, stride, lane)
+            low_p = low_v if k == 0 else lows(p_of, stride, lane)
+            high_s = highs(s_of, stride, lane)
             for t in range(TILES):
-                e, e_low, e_high = next(lows)
-                f, f_low, f_high = next(highs)
-                q = 1.0 / (1.0 - e * f_low - f * e_high)
-                pivot[k, tile(h, t), :] = q
+                v = next(low_v)
+                high = next(high_s)
+                if k == 0:
+                    b = v
+                    if t == 0:
+                        b = jnp.where(lane < 2, 0.0, v)
+                        v = jnp.where(lane < 1, 0.0, v)
+                    if t == TILES - 1:
+                        high = jnp.where(lane == LANES - 1, 0.0, high)
+                else:
+                    b = couple[k, tile(h, t), :]
+                    v = b * b * v
+                    b = b * next(low_p)
+                m = main[now, tile(h, t), :] - v - high
+                main[1 - now, tile(h, t), :] = m
+                couple[k + 1, tile(h, t), :] = b
                 if k < STEPS - 1:
-                    lower[k + 1, tile(h, t), :] = e * e_low * q
-                    upper[k + 1, tile(h, t), :] = f * f_high * q
+                    inv[k + 1, tile(h, t), :] = 1.0 / m
+    for h in range(HALVES):
+        a = b = 0.0
+        below_b = couple[STEPS, tile(h, 0), :]
+        ends = [below_b]
+        for step in range(MID):
+            t = step
+            e = ends.pop()
+            f = couple[STEPS, tile(h, t + 1), :]
+            ends.append(f)
+            q = 1.0 / (main[STEPS % 2, tile(h, t), :] - e * b)
+            inv[STEPS, tile(h, t), :] = q
+            couple[STEPS, tile(h, t), :] = e * q
+            b = f * q
+            upper[tile(h, t), :] = b
+            t = TILES - 1 - step
+            e = couple[STEPS, tile(h, t), :]
+            f = below_b
+            below_b = e
+            q = 1.0 / (main[STEPS % 2, tile(h, t), :] - f * a)
+            inv[STEPS, tile(h, t), :] = q
+            a = e * q
+            couple[STEPS, tile(h, t), :] = a
+            upper[tile(h, t), :] = f * q
+        centre[pl.ds(h * SUB, SUB), :] = 1.0 / (1.0 - b * a)
 
     scale = history_weights()
     copies[1].wait()
-    copies[2].wait()
     for h in range(HALVES):
         rows = slice(h * SUB, (h + 1) * SUB)
-        for t in range(TILES):
-            tgt_l[tile(h, t), :] = tgt[rows, t * LANES:(t + 1) * LANES]
-    for h in range(HALVES):
-        rows = slice(h * SUB, (h + 1) * SUB)
+        if h == HALVES - 1:
+            late.wait()
+            for i in range(VREGS):
+                g = i // TILES
+                t = i % TILES
+                tgt_l[tile(g, t), :] = tgt[g * SUB:(g + 1) * SUB, t * LANES:(t + 1) * LANES]
         for c in range(CHUNKS):
-            copies[3 + h * CHUNKS + c].wait()
+            copies[2 + h * CHUNKS + c].wait()
             for t in range(c * CHUNK_TILES, (c + 1) * CHUNK_TILES):
                 cols = slice(t * LANES, (t + 1) * LANES)
                 acc = src[rows, cols]
@@ -171,16 +221,43 @@
                 rhs[0, tile(h, t), :] = acc * first[tile(h, t), :]
         for k in range(STEPS):
             now = k % 2
-            values = neighbours(lambda t: rhs[now, tile(h, t), :], 1 << k, lane)
+
+            def z_of(t):
+                return inv[k, tile(h, t), :] * rhs[now, tile(h, t), :]
+
+            def y_of(t):
+                return z_of(t) if k == 0 else couple[k, tile(h, t), :] * z_of(t)
+
+            low_z = lows(z_of, 1 << k, lane)
+            high_y = highs(y_of, 1 << k, lane)
             for t in range(TILES):
-                d, low, high = next(values)
-                d = (
-                    d + lower[k, tile(h, t), :] * low + upper[k, tile(h, t), :] * high
-                ) * pivot[k, tile(h, t), :]
-                if k < STEPS - 1:
-                    rhs[1 - now, tile(h, t), :] = d
-                else:
-                    sw_l[tile(h, t), :] = d
+                low = next(low_z)
+                high = next(high_y)
+                if k:
+                    low = couple[k, tile(h, t), :] * low
+                elif t == 0:
+                    low = jnp.where(lane == 0, 0.0, low)
+                elif t == TILES - 1:
+                    high = jnp.where(lane == LANES - 1, 0.0, high)
+                rhs[1 - now, tile(h, t), :] = rhs[now, tile(h, t), :] + low + high
+        d = [inv[STEPS, tile(h, t), :] * rhs[STEPS % 2, tile(h, t), :] for t in range(TILES)]
+        for step in range(1, MID):
+            t = step
+            d[t] = d[t] + couple[STEPS, tile(h, t), :] * d[t - 1]
+            t = TILES - 1 - step
+            d[t] = d[t] + upper[tile(h, t), :] * d[t + 1]
+        x = d[MID - 1] + upper[tile(h, MID - 1), :] * d[MID]
+        x = x * centre[pl.ds(h * SUB, SUB), :]
+        y = d[MID] + couple[STEPS, tile(h, MID), :] * x
+        sw_l[tile(h, MID - 1), :] = x
+        sw_l[tile(h, MID), :] = y
+        for step in range(1, MID):
+            t = MID - 1 - step
+            x = d[t] + upper[tile(h, t), :] * x
+            sw_l[tile(h, t), :] = x
+            t = MID + step
+            y = d[t] + couple[STEPS, tile(h, t), :] * y
+            sw_l[tile(h, t), :] = y
 
     p = None
     for r in range(ROWS):
@@ -274,7 +351,8 @@
     block = pltpu.VMEM((ROWS, NY), F32)
     tiles = pltpu.VMEM((VREGS * SUB, LANES), F32)
     pair = pltpu.VMEM((2, VREGS * SUB, LANES), F32)
-    stages = pltpu.VMEM((STEPS, VREGS * SUB, LANES), F32)
+    stages = pltpu.VMEM((STEPS + 1, VREGS * SUB, LANES), F32)
+    block_tile = pltpu.VMEM((ROWS, LANES), F32)
     lines = INNER * TILES
     params = pltpu.CompilerParams(vmem_limit_bytes=48 * 1024 * 1024)
     msg, part, above, below = pl.pallas_call(
@@ -285,7 +363,7 @@
         out_specs=[vmem] * 4,
         scratch_shapes=[
             pltpu.VMEM((LEVELS, ROWS, NY), F32), block, block, block,
-            stages, stages, stages, tiles, pair,
+            stages, stages, pair, tiles, tiles, block_tile, pair,
             tiles, tiles, tiles, tiles, tiles, tiles, tiles,
             pltpu.SemaphoreType.DMA((3 + HALVES * CHUNKS,)),
         ],

time: 44.8 us -> 44.2 us (0.987)
  Pallas kernels: 7.88 us -> 7.28 us
    pallas_call x1, Pallas kernels: 5.95 us -> 5.35 us  [body(): pl.pallas_call(local_kernel, name='local', out_shape=[shape((4 * BLOCKS,...]
where the time goes in v4:
time: 44.2 us; the launch traced here: 44.1 us
  blocking collectives  36.1 us (82%)
  Pallas kernels  7.28 us (16%)
  between operations  0.65 us (1%)
    all_to_all x1, blocking collectives, body(): lax.all_to_all(msg.reshape(BLOCKS, 4, LANES), AXIS, split_axis=0, concat_...  22.2 us
    all_to_all x1, blocking collectives, body(): solved = lax.all_to_all(back, AXIS, split_axis=0, concat_axis=0, tiled=True)  14 us
    pallas_call x1, Pallas kernels, body(): pl.pallas_call(local_kernel, name='local', out_shape=[shape((4 * BLOCKS,...  5.35 us
    pallas_call x1, Pallas kernels, body(): pl.pallas_call(reduced_kernel, name='reduced', out_shape=shape((BLOCKS, L...  1.06 us

profile of v4, /device:TPU:1, one launch (start us, length us, event | category | flops | bytes accessed | tf_op | source)
XLA Modules:
  0.0 44.1 jit_solution(17432625092319481158)
XLA Ops:
  0.6 5.4 %local.1 = (f32[512,128]{1,0:T(8,128)S(1)}, f32[480,128]{1,0:T(8,128)S(1)}, f32[480,128]{1,0:T(8,128)S(1)}, f32[480,128]{1,0:T(8,128)S(1)}) custom-call(f32[32,16,4096]{2,1,0:T(8,128)} %hist_hbm.1, f32[16,4096]{1,0:T(8,128)} %src_hbm.1, f32[16,4096]{1,0:T(8,128)} %dif_hbm.1, f32[16,4096]{1,0:T(8,128)} %tgt_hbm.1), custom_call_target="tpu_custom_call" | custom-call | tf_op jit(solution)/shard_map/local/pallas_call | solution.py:358
  6.0 22.2 %all_to_all.16 = f32[128,4,128]{2,1,0:T(4,128)S(1)} all-to-all(f32[128,4,128]{2,1,0:T(4,128)S(1)} %bitcast.9), channel_id=1, replica_groups=mesh['rows'=128] {'rows'}, dimensions={0} | all-to-all | bytes 524288 | tf_op jit(solution)/shard_map/all_to_all | solution.py:372
  28.2 1.1 %reduced.1 = f32[128,128]{1,0:T(8,128)S(1)} custom-call(f32[512,128]{1,0:T(8,128)S(1)} %bitcast.6), custom_call_target="tpu_custom_call" | custom-call | tf_op jit(solution)/shard_map/reduced/pallas_call | solution.py:375
  29.2 14.0 %all_to_all.17 = f32[128,1,128]{2,1,0:T(1,128)S(1)} all-to-all(f32[128,1,128]{2,1,0:T(1,128)S(1)} %bitcast.8), channel_id=1, replica_groups=mesh['rows'=128] {'rows'}, dimensions={0} | all-to-all | bytes 131072 | tf_op jit(solution)/shard_map/all_to_all | solution.py:383
  43.2 0.9 %final.1 = (f32[16,4096]{1,0:T(8,128)}, f32[2]{0:T(128)}) custom-call(f32[128,128]{1,0:T(8,128)S(1)} %bitcast.7, f32[480,128]{1,0:T(8,128)S(1)} %get-tuple-element.7.part, f32[480,128]{1,0:T(8,128)S(1)} %get-tuple-element.8.above, f32[480,128]{1,0:T(8,128)S(1)} %get-tuple-element.9.below), custom_call_target="tpu_custom_call" | custom-call | tf_op jit(solution)/shard_map/final/pallas_call | solution.py:384

commit v5 on v4

--- a/solution.py
+++ b/solution.py
@@ -64,13 +64,28 @@
         here = after
 
 
+def both(load, lane):
+    half = LANES // 2
+    last = before = pltpu.roll(load(TILES - 1), half, 1)
+    first = here = pltpu.roll(load(0), half, 1)
+    for t in range(TILES):
+        if t == TILES - 1:
+            after = first
+        elif t == TILES - 2:
+            after = last
+        else:
+            after = pltpu.roll(load(t + 1), half, 1)
+        yield jnp.where(lane < half, before, here), jnp.where(lane >= half, after, here)
+        before, here = here, after
+
+
 def local_kernel(
     hist_hbm, src_hbm, dif_hbm, tgt_hbm,
     msg, part, above, below,
     hist, src, dif, tgt,
-    couple, inv, main, upper, first, centre, rhs,
+    couple, inv, main, upper, beyond, first, centre, rhs,
     dif_l, tgt_l, sw_l, gg, hh, rr, pp,
-    sems,
+    weights, sems,
 ):
     copies = [
         pltpu.make_async_copy(dif_hbm, dif, sems.at[0]),
@@ -92,6 +107,8 @@
         if i == CHUNKS + 1:
             late.start()
     lane = lax.broadcasted_iota(jnp.int32, (SUB, LANES), 1)
+    for k, value in enumerate(history_weights()):
+        weights[pl.ds(k * SUB, SUB), :] = jnp.full((SUB, LANES), value, F32)
 
     copies[0].wait()
     for h in range(HALVES):
@@ -100,9 +117,9 @@
             dif_l[tile(h, t), :] = c
             q = 1.0 / c
             first[tile(h, t), :] = q
-            m = 2.0 + q
-            main[0, tile(h, t), :] = m
-            inv[0, tile(h, t), :] = 1.0 / m
+            u = 0.5 * q * (1.0 / (2.0 + q))
+            couple[0, tile(h, t), :] = u
+            inv[0, tile(h, t), :] = 0.5 - u
 
     g = h_ = None
     for r in range(ROWS):
@@ -141,42 +158,57 @@
     send(0, [a, b, hh[wide(INNER), :], gg[wide(INNER), :]])
     send(1, [sum_a, sum_b + 1.0, sum_aa, sum_ab])
 
-    for k in range(STEPS):
-        stride = 1 << k
-        now = k % 2
-        for h in range(HALVES):
+    def bands(h):
+        low_u = lows(lambda t: couple[0, tile(h, t), :], 1, lane)
+        high_u = highs(lambda t: couple[0, tile(h, t), :], 1, lane)
+        for t in range(TILES):
+            low = next(low_u)
+            high = next(high_u)
+            q = first[tile(h, t), :]
+            m = 1.0 + (q + low + high)
+            b = 0.5 - low
+            if t == 0:
+                m = jnp.where(lane == 0, 1.5 + (q + high), m)
+                b = jnp.where(lane < 2, 0.0, b)
+            if t == TILES - 1:
+                m = jnp.where(lane == LANES - 1, 1.5 + (q + low), m)
+            main[1, tile(h, t), :] = m
+            couple[1, tile(h, t), :] = b
+            inv[1, tile(h, t), :] = 1.0 / m
+            yield
+        for k in range(1, STEPS):
+            stride = 1 << k
+            now = k % 2
+
             def v_of(t):
                 return inv[k, tile(h, t), :]
 
             def p_of(t):
-                return v_of(t) if k == 0 else couple[k, tile(h, t), :] * v_of(t)
-
-            def s_of(t):
-                return v_of(t) if k == 0 else couple[k, tile(h, t), :] * p_of(t)
-
+                return couple[k, tile(h, t), :] * v_of(t)
+
+            if k == STEPS - 1:
+                pairs_v = both(v_of, lane)
+                pairs_b = both(lambda t: couple[k, tile(h, t), :], lane)
+                for t in range(TILES):
+                    b = couple[k, tile(h, t), :]
+                    low_v, high_v = next(pairs_v)
+                    low_b, high_b = next(pairs_b)
+                    beyond[tile(h, t), :] = high_b
+                    m = main[now, tile(h, t), :] - b * b * low_v - high_b * high_b * high_v
+                    main[1 - now, tile(h, t), :] = m
+                    couple[k + 1, tile(h, t), :] = b * low_b * low_v
+                    yield
+                continue
             low_v = lows(v_of, stride, lane)
-            low_p = low_v if k == 0 else lows(p_of, stride, lane)
-            high_s = highs(s_of, stride, lane)
+            low_p = lows(p_of, stride, lane)
+            high_s = highs(lambda t: couple[k, tile(h, t), :] * p_of(t), stride, lane)
             for t in range(TILES):
-                v = next(low_v)
-                high = next(high_s)
-                if k == 0:
-                    b = v
-                    if t == 0:
-                        b = jnp.where(lane < 2, 0.0, v)
-                        v = jnp.where(lane < 1, 0.0, v)
-                    if t == TILES - 1:
-                        high = jnp.where(lane == LANES - 1, 0.0, high)
-                else:
-                    b = couple[k, tile(h, t), :]
-                    v = b * b * v
-                    b = b * next(low_p)
-                m = main[now, tile(h, t), :] - v - high
+                b = couple[k, tile(h, t), :]
+                m = main[now, tile(h, t), :] - b * b * next(low_v) - next(high_s)
                 main[1 - now, tile(h, t), :] = m
-                couple[k + 1, tile(h, t), :] = b
-                if k < STEPS - 1:
-                    inv[k + 1, tile(h, t), :] = 1.0 / m
-    for h in range(HALVES):
+                couple[k + 1, tile(h, t), :] = b * next(low_p)
+                inv[k + 1, tile(h, t), :] = 1.0 / m
+                yield
         a = b = 0.0
         below_b = couple[STEPS, tile(h, 0), :]
         ends = [below_b]
@@ -199,26 +231,21 @@
             a = e * q
             couple[STEPS, tile(h, t), :] = a
             upper[tile(h, t), :] = f * q
+            yield
         centre[pl.ds(h * SUB, SUB), :] = 1.0 / (1.0 - b * a)
 
-    scale = history_weights()
-    copies[1].wait()
-    for h in range(HALVES):
+    def drive(h, c):
         rows = slice(h * SUB, (h + 1) * SUB)
-        if h == HALVES - 1:
-            late.wait()
-            for i in range(VREGS):
-                g = i // TILES
-                t = i % TILES
-                tgt_l[tile(g, t), :] = tgt[g * SUB:(g + 1) * SUB, t * LANES:(t + 1) * LANES]
-        for c in range(CHUNKS):
-            copies[2 + h * CHUNKS + c].wait()
-            for t in range(c * CHUNK_TILES, (c + 1) * CHUNK_TILES):
-                cols = slice(t * LANES, (t + 1) * LANES)
-                acc = src[rows, cols]
-                for k in range(LEVELS):
-                    acc = acc + scale[k] * hist[k, rows, cols]
-                rhs[0, tile(h, t), :] = acc * first[tile(h, t), :]
+        own = range(c * CHUNK_TILES, (c + 1) * CHUNK_TILES)
+        acc = [src[rows, t * LANES:(t + 1) * LANES] for t in own]
+        for k in range(LEVELS):
+            weight = weights[pl.ds(k * SUB, SUB), :]
+            for i, t in enumerate(own):
+                acc[i] = acc[i] + weight * hist[k, rows, t * LANES:(t + 1) * LANES]
+        for i, t in enumerate(own):
+            rhs[0, tile(h, t), :] = acc[i] * first[tile(h, t), :]
+
+    def right_side(h):
         for k in range(STEPS):
             now = k % 2
 
@@ -228,6 +255,14 @@
             def y_of(t):
                 return z_of(t) if k == 0 else couple[k, tile(h, t), :] * z_of(t)
 
+            if k == STEPS - 1:
+                pairs_z = both(z_of, lane)
+                for t in range(TILES):
+                    low, high = next(pairs_z)
+                    low = couple[k, tile(h, t), :] * low
+                    high = beyond[tile(h, t), :] * high
+                    rhs[1 - now, tile(h, t), :] = rhs[now, tile(h, t), :] + low + high
+                continue
             low_z = lows(z_of, 1 << k, lane)
             high_y = highs(y_of, 1 << k, lane)
             for t in range(TILES):
@@ -259,6 +294,25 @@
             y = d[t] + couple[STEPS, tile(h, t), :] * y
             sw_l[tile(h, t), :] = y
 
+    halves = [bands(h) for h in range(HALVES)]
+    for k in range(STEPS + 1):
+        for half in halves:
+            for _ in range(TILES):
+                next(half, None)
+
+    copies[1].wait()
+    for h in range(HALVES):
+        if h == HALVES - 1:
+            late.wait()
+            for i in range(VREGS):
+                g = i // TILES
+                t = i % TILES
+                tgt_l[tile(g, t), :] = tgt[g * SUB:(g + 1) * SUB, t * LANES:(t + 1) * LANES]
+        for c in range(CHUNKS):
+            copies[2 + h * CHUNKS + c].wait()
+            drive(h, c)
+        right_side(h)
+
     p = None
     for r in range(ROWS):
         s = rr[wide(r), :] * sw_l[line(r), :]
@@ -363,8 +417,9 @@
         out_specs=[vmem] * 4,
         scratch_shapes=[
             pltpu.VMEM((LEVELS, ROWS, NY), F32), block, block, block,
-            stages, stages, pair, tiles, tiles, block_tile, pair,
+            stages, stages, pair, tiles, tiles, tiles, block_tile, pair,
             tiles, tiles, tiles, tiles, tiles, tiles, tiles,
+            pltpu.VMEM((LEVELS * SUB, LANES), F32),
             pltpu.SemaphoreType.DMA((3 + HALVES * CHUNKS,)),
         ],
         compiler_params=params,

time: 44.2 us -> 44 us (level)
  no operation moved by 1% of the time
where the time goes in v5:
time: 44 us; the launch traced here: 43.9 us
  blocking collectives  36.1 us (82%)
  Pallas kernels  7.1 us (16%)
  between operations  0.65 us (1%)
    all_to_all x1, blocking collectives, body(): lax.all_to_all(msg.reshape(BLOCKS, 4, LANES), AXIS, split_axis=0, concat_...  22.2 us
    all_to_all x1, blocking collectives, body(): solved = lax.all_to_all(back, AXIS, split_axis=0, concat_axis=0, tiled=True)  14 us
    pallas_call x1, Pallas kernels, body(): pl.pallas_call(local_kernel, name='local', out_shape=[shape((4 * BLOCKS,...  5.17 us
    pallas_call x1, Pallas kernels, body(): pl.pallas_call(reduced_kernel, name='reduced', out_shape=shape((BLOCKS, L...  1.06 us

profile of v5, /device:TPU:1, one launch (start us, length us, event | category | flops | bytes accessed | tf_op | source)
XLA Modules:
  0.0 43.9 jit_solution(3115145301122110137)
XLA Ops:
  0.6 5.2 %local.1 = (f32[512,128]{1,0:T(8,128)S(1)}, f32[480,128]{1,0:T(8,128)S(1)}, f32[480,128]{1,0:T(8,128)S(1)}, f32[480,128]{1,0:T(8,128)S(1)}) custom-call(f32[32,16,4096]{2,1,0:T(8,128)} %hist_hbm.1, f32[16,4096]{1,0:T(8,128)} %src_hbm.1, f32[16,4096]{1,0:T(8,128)} %dif_hbm.1, f32[16,4096]{1,0:T(8,128)} %tgt_hbm.1), custom_call_target="tpu_custom_call" | custom-call | tf_op jit(solution)/shard_map/local/pallas_call | solution.py:412
  5.8 22.2 %all_to_all.16 = f32[128,4,128]{2,1,0:T(4,128)S(1)} all-to-all(f32[128,4,128]{2,1,0:T(4,128)S(1)} %bitcast.9), channel_id=1, replica_groups=mesh['rows'=128] {'rows'}, dimensions={0} | all-to-all | bytes 524288 | tf_op jit(solution)/shard_map/all_to_all | solution.py:427
  28.0 1.1 %reduced.1 = f32[128,128]{1,0:T(8,128)S(1)} custom-call(f32[512,128]{1,0:T(8,128)S(1)} %bitcast.6), custom_call_target="tpu_custom_call" | custom-call | tf_op jit(solution)/shard_map/reduced/pallas_call | solution.py:430
  29.1 14.0 %all_to_all.17 = f32[128,1,128]{2,1,0:T(1,128)S(1)} all-to-all(f32[128,1,128]{2,1,0:T(1,128)S(1)} %bitcast.8), channel_id=1, replica_groups=mesh['rows'=128] {'rows'}, dimensions={0} | all-to-all | bytes 131072 | tf_op jit(solution)/shard_map/all_to_all | solution.py:438
  43.0 0.9 %final.1 = (f32[16,4096]{1,0:T(8,128)}, f32[2]{0:T(128)}) custom-call(f32[128,128]{1,0:T(8,128)S(1)} %bitcast.7, f32[480,128]{1,0:T(8,128)S(1)} %get-tuple-element.7.part, f32[480,128]{1,0:T(8,128)S(1)} %get-tuple-element.8.above, f32[480,128]{1,0:T(8,128)S(1)} %get-tuple-element.9.below), custom_call_target="tpu_custom_call" | custom-call | tf_op jit(solution)/shard_map/final/pallas_call | solution.py:439

commit v6 on v5

--- a/solution.py
+++ b/solution.py
@@ -340,47 +340,73 @@
     send(3, [sum_da, sum_db, sum_bb + 1.0, zero])
 
 
-def reduced_kernel(got, back):
-    groups = [got[pl.ds(g, BLOCKS, stride=4), :].T for g in range(4)]
-    q = [groups[i // 4][(i % 4) * TILES:(i % 4 + 1) * TILES] for i in range(15)]
-    (a0, b0, u, v, sum_a, sum_b, sum_aa, sum_ab, p0, w, sum_p, sum_dd, sum_da, sum_db, sum_bb) = q
-    lane = lax.broadcasted_iota(jnp.int32, (TILES, LANES), 1)
-    u = jnp.where(lane == 0, 0.0, u)
-    v = jnp.where(lane == BLOCKS - 1, 0.0, v)
-
-    def low(x, s):
-        return pltpu.roll(x, s, 1)
-
-    def high(x, s):
-        return pltpu.roll(x, LANES - s, 1)
-
-    r = 1.0 / (1.0 - v * high(a0, 1))
+def reduced_kernel(got, back, left, right, value):
+    groups = [got[pl.ds(g, BLOCKS, stride=4), :] for g in range(4)]
+    edge = jnp.zeros((SUB, LANES), F32)
+    for ref in (left, right, value):
+        ref[pl.ds(0, SUB), :] = edge
+        ref[pl.ds(SUB + BLOCKS, SUB), :] = edge
+    inside = pl.ds(SUB, BLOCKS)
+
+    def low(x, ref, s):
+        if s < SUB:
+            return ref[pl.ds(SUB - s, BLOCKS), :]
+        return jnp.concatenate([jnp.zeros((s, LANES), F32), x[:BLOCKS - s]], axis=0)
+
+    def high(x, ref, s):
+        if s < SUB:
+            return ref[pl.ds(SUB + s, BLOCKS), :]
+        return jnp.concatenate([x[s:], jnp.zeros((s, LANES), F32)], axis=0)
+
+    lane = lax.broadcasted_iota(jnp.int32, (BLOCKS, LANES), 1)
+    row = lax.broadcasted_iota(jnp.int32, (BLOCKS, LANES), 0)
+    left[inside, :] = groups[0]
+    right[inside, :] = pltpu.roll(groups[0], LANES - TILES, 1)
+    value[inside, :] = groups[2]
+    u = jnp.where(row == 0, 0.0, pltpu.roll(groups[0], LANES - 2 * TILES, 1))
+    v = jnp.where(row == BLOCKS - 1, 0.0, pltpu.roll(groups[0], LANES - 3 * TILES, 1))
+    w = pltpu.roll(groups[2], LANES - TILES, 1)
+    r = 1.0 / (1.0 - v * high(None, left, 1))
     e = u * r
-    f = v * high(b0, 1) * r
-    d = (w + v * high(p0, 1)) * r
+    f = v * high(None, right, 1) * r
+    d = (w + v * high(None, value, 1)) * r
     s = 1
     while s < BLOCKS:
-        r = 1.0 / (1.0 - e * low(f, s) - f * high(e, s))
-        d = (d + e * low(d, s) + f * high(d, s)) * r
+        if s < SUB:
+            left[inside, :] = e
+            right[inside, :] = f
+            value[inside, :] = d
+        r = 1.0 / (1.0 - e * low(f, right, s) - f * high(e, left, s))
+        d = (d + e * low(d, value, s) + f * high(d, value, s)) * r
         if 2 * s < BLOCKS:
-            e, f = e * low(e, s) * r, f * high(f, s) * r
+            e, f = e * low(e, left, s) * r, f * high(f, right, s) * r
         s *= 2
     z = d
-    x = jnp.where(lane == 0, 0.0, low(z, 1))
-    mass = sum_p + sum_a * x + sum_b * z
+    for g in range(1, 4):
+        z = jnp.where(lane >= g * TILES, pltpu.roll(d, g * TILES, 1), z)
+    value[inside, :] = z
+    x = low(None, value, 1)
+    part = lane[:1] // TILES
+    square = groups[1] * jnp.where(
+        lane < TILES, x, jnp.where(lane < 2 * TILES, z, x * jnp.where(lane < 3 * TILES, x, z))
+    )
+    cross = groups[3] * jnp.where(lane < TILES, x, jnp.where(lane < 2 * TILES, z, z * z))
+
+    def rows(y):
+        return jnp.sum(y, axis=0, keepdims=True)
+
+    square, cross, plain = rows(square), rows(cross), rows(groups[2])
+    mass = jnp.where(part < 2, square, jnp.where(part == 2, plain, 0.0))
     error = (
-        sum_dd
-        + 2.0 * (sum_da * x + sum_db * z + sum_ab * x * z)
-        + sum_aa * x * x
-        + sum_bb * z * z
+        jnp.where(part == 2, square, jnp.where(part == 3, 2.0 * square + plain, 0.0))
+        + jnp.where(part < 2, 2.0 * cross, jnp.where(part == 2, cross, 0.0))
     )
-
-    def total(y):
-        y = jnp.sum(jnp.sum(y, axis=0, keepdims=True), axis=1, keepdims=True)
-        return jnp.broadcast_to(y, (SUB, LANES))
-
-    rest = jnp.zeros((LANES - 2 * TILES - 2 * SUB, LANES), F32)
-    back[...] = jnp.concatenate([z, x, total(mass), total(error), rest], axis=0).T
+    mass = jnp.sum(mass, axis=1, keepdims=True)
+    error = jnp.sum(error, axis=1, keepdims=True)
+    totals = jnp.where(part == 2, mass, error)
+    back[...] = jnp.where(
+        lane < TILES, z, jnp.where(lane < 2 * TILES, x, jnp.broadcast_to(totals, (BLOCKS, LANES)))
+    )
 
 
 def final_kernel(got, part, above, below, update, totals, lines):
@@ -389,7 +415,7 @@
     x = t[TILES:2 * TILES]
     scale = 1.0 / (BLOCKS * ROWS * NY)
     totals[0] = jnp.sum(t[2 * TILES:2 * TILES + 1]) * scale
-    totals[1] = jnp.sum(t[2 * TILES + SUB:2 * TILES + SUB + 1]) * scale
+    totals[1] = jnp.sum(t[3 * TILES:3 * TILES + 1]) * scale
     for r in range(INNER):
         lines[line(r), :] = part[wide(r), :] + above[wide(r), :] * x + below[wide(r), :] * z
     lines[line(INNER), :] = z
@@ -433,6 +459,7 @@
         out_shape=shape((BLOCKS, LANES), F32),
         in_specs=[vmem],
         out_specs=vmem,
+        scratch_shapes=[pltpu.VMEM((BLOCKS + 2 * SUB, LANES), F32)] * 3,
         compiler_params=params,
     )(got)
     solved = lax.all_to_all(back, AXIS, split_axis=0, concat_axis=0, tiled=True)

time: 44 us -> 43.5 us (0.989)
  Pallas kernels: 7.1 us -> 6.61 us
    pallas_call x1, Pallas kernels: 1.06 us -> 0.57 us  [body(): pl.pallas_call(reduced_kernel, name='reduced', out_shape=shape((BLOCKS, L...]
where the time goes in v6:
time: 43.5 us; the launch traced here: 43.4 us
  blocking collectives  36.1 us (83%)
  Pallas kernels  6.61 us (15%)
  between operations  0.64 us (1%)
    all_to_all x1, blocking collectives, body(): lax.all_to_all(msg.reshape(BLOCKS, 4, LANES), AXIS, split_axis=0, concat_...  22.2 us
    all_to_all x1, blocking collectives, body(): solved = lax.all_to_all(back, AXIS, split_axis=0, concat_axis=0, tiled=True)  14 us
    pallas_call x1, Pallas kernels, body(): pl.pallas_call(local_kernel, name='local', out_shape=[shape((4 * BLOCKS,...  5.17 us

profile of v6, /device:TPU:1, one launch (start us, length us, event | category | flops | bytes accessed | tf_op | source)
XLA Modules:
  0.0 43.4 jit_solution(5600166443656776132)
XLA Ops:
  0.6 5.2 %local.1 = (f32[512,128]{1,0:T(8,128)S(1)}, f32[480,128]{1,0:T(8,128)S(1)}, f32[480,128]{1,0:T(8,128)S(1)}, f32[480,128]{1,0:T(8,128)S(1)}) custom-call(f32[32,16,4096]{2,1,0:T(8,128)} %hist_hbm.1, f32[16,4096]{1,0:T(8,128)} %src_hbm.1, f32[16,4096]{1,0:T(8,128)} %dif_hbm.1, f32[16,4096]{1,0:T(8,128)} %tgt_hbm.1), custom_call_target="tpu_custom_call" | custom-call | tf_op jit(solution)/shard_map/local/pallas_call | solution.py:438
  5.8 22.2 %all_to_all.16 = f32[128,4,128]{2,1,0:T(4,128)S(1)} all-to-all(f32[128,4,128]{2,1,0:T(4,128)S(1)} %bitcast.9), channel_id=1, replica_groups=mesh['rows'=128] {'rows'}, dimensions={0} | all-to-all | bytes 524288 | tf_op jit(solution)/shard_map/all_to_all | solution.py:453
  28.0 0.6 %reduced.1 = f32[128,128]{1,0:T(8,128)S(1)} custom-call(f32[512,128]{1,0:T(8,128)S(1)} %bitcast.6), custom_call_target="tpu_custom_call" | custom-call | tf_op jit(solution)/shard_map/reduced/pallas_call | solution.py:456
  28.6 14.0 %all_to_all.17 = f32[128,1,128]{2,1,0:T(1,128)S(1)} all-to-all(f32[128,1,128]{2,1,0:T(1,128)S(1)} %bitcast.8), channel_id=1, replica_groups=mesh['rows'=128] {'rows'}, dimensions={0} | all-to-all | bytes 131072 | tf_op jit(solution)/shard_map/all_to_all | solution.py:465
  42.5 0.9 %final.1 = (f32[16,4096]{1,0:T(8,128)}, f32[2]{0:T(128)}) custom-call(f32[128,128]{1,0:T(8,128)S(1)} %bitcast.7, f32[480,128]{1,0:T(8,128)S(1)} %get-tuple-element.7.part, f32[480,128]{1,0:T(8,128)S(1)} %get-tuple-element.8.above, f32[480,128]{1,0:T(8,128)S(1)} %get-tuple-element.9.below), custom_call_target="tpu_custom_call" | custom-call | tf_op jit(solution)/shard_map/final/pallas_call | solution.py:466

commit v7 on v6

--- a/solution.py
+++ b/solution.py
@@ -19,8 +19,9 @@
 VREGS = HALVES * TILES
 BLOCKS = 128
 INNER = ROWS - 1
-CHUNKS = 4
-CHUNK_TILES = TILES // CHUNKS
+CHUNK_TILES = 8
+PIECES = ((0, 16, 32), (0, 16, 32))
+COPIES = 3 + sum(len(cuts) - 1 for cuts in PIECES)
 STEPS = 7
 MID = TILES // 2
 F32 = jnp.float32
@@ -87,25 +88,24 @@
     dif_l, tgt_l, sw_l, gg, hh, rr, pp,
     weights, sems,
 ):
+    def piece(h, k, sem):
+        rows = pl.ds(h * SUB, SUB)
+        cols = pl.ds(PIECES[h][k] * LANES, (PIECES[h][k + 1] - PIECES[h][k]) * LANES)
+        return pltpu.make_async_copy(hist_hbm.at[:, rows, cols], hist.at[:, rows, cols], sem)
+
     copies = [
         pltpu.make_async_copy(dif_hbm, dif, sems.at[0]),
         pltpu.make_async_copy(src_hbm, src, sems.at[1]),
+        pltpu.make_async_copy(tgt_hbm, tgt, sems.at[2]),
     ]
-    late = pltpu.make_async_copy(tgt_hbm, tgt, sems.at[HALVES * CHUNKS + 2])
-    width = CHUNK_TILES * LANES
+    pieces = []
     for h in range(HALVES):
-        rows = pl.ds(h * SUB, SUB)
-        for c in range(CHUNKS):
-            cols = pl.ds(c * width, width)
-            copies.append(
-                pltpu.make_async_copy(
-                    hist_hbm.at[:, rows, cols], hist.at[:, rows, cols], sems.at[len(copies)]
-                )
-            )
-    for i, copy in enumerate(copies):
+        pieces.append([])
+        for k in range(len(PIECES[h]) - 1):
+            copies.append(piece(h, k, sems.at[len(copies)]))
+            pieces[h].append(copies[-1])
+    for copy in [*copies[:2], *pieces[0], copies[2], *pieces[1]]:
         copy.start()
-        if i == CHUNKS + 1:
-            late.start()
     lane = lax.broadcasted_iota(jnp.int32, (SUB, LANES), 1)
     for k, value in enumerate(history_weights()):
         weights[pl.ds(k * SUB, SUB), :] = jnp.full((SUB, LANES), value, F32)
@@ -301,23 +301,23 @@
                 next(half, None)
 
     copies[1].wait()
+    p = None
     for h in range(HALVES):
         if h == HALVES - 1:
-            late.wait()
+            copies[2].wait()
             for i in range(VREGS):
                 g = i // TILES
                 t = i % TILES
                 tgt_l[tile(g, t), :] = tgt[g * SUB:(g + 1) * SUB, t * LANES:(t + 1) * LANES]
-        for c in range(CHUNKS):
-            copies[2 + h * CHUNKS + c].wait()
+        for c in range(TILES // CHUNK_TILES):
+            if c * CHUNK_TILES in PIECES[h]:
+                pieces[h][PIECES[h].index(c * CHUNK_TILES)].wait()
             drive(h, c)
         right_side(h)
-
-    p = None
-    for r in range(ROWS):
-        s = rr[wide(r), :] * sw_l[line(r), :]
-        p = s if r == 0 else s + gg[wide(r), :] * p
-        pp[wide(r), :] = p
+        for r in range(h * SUB, (h + 1) * SUB):
+            s = rr[wide(r), :] * sw_l[line(r), :]
+            p = s if r == 0 else s + gg[wide(r), :] * p
+            pp[wide(r), :] = p
     tip = p
     d = tgt_l[line(INNER), :]
     sum_dd = d * d
@@ -409,7 +409,7 @@
     )
 
 
-def final_kernel(got, part, above, below, update, totals, lines):
+def final_kernel(got, part, above, below, update, totals):
     t = got[...].T
     z = t[:TILES]
     x = t[TILES:2 * TILES]
@@ -417,11 +417,8 @@
     totals[0] = jnp.sum(t[2 * TILES:2 * TILES + 1]) * scale
     totals[1] = jnp.sum(t[3 * TILES:3 * TILES + 1]) * scale
     for r in range(INNER):
-        lines[line(r), :] = part[wide(r), :] + above[wide(r), :] * x + below[wide(r), :] * z
-    lines[line(INNER), :] = z
-    for h in range(HALVES):
-        for i in range(TILES):
-            update[h * SUB:(h + 1) * SUB, i * LANES:(i + 1) * LANES] = lines[tile(h, i), :]
+        update[line(r), :] = part[wide(r), :] + above[wide(r), :] * x + below[wide(r), :] * z
+    update[line(INNER), :] = z
 
 
 def body(history, source, diffusivity, target):
@@ -446,7 +443,7 @@
             stages, stages, pair, tiles, tiles, tiles, block_tile, pair,
             tiles, tiles, tiles, tiles, tiles, tiles, tiles,
             pltpu.VMEM((LEVELS * SUB, LANES), F32),
-            pltpu.SemaphoreType.DMA((3 + HALVES * CHUNKS,)),
+            pltpu.SemaphoreType.DMA((COPIES,)),
         ],
         compiler_params=params,
     )(*(pltpu.with_memory_space_constraint(x, pltpu.HBM) for x in (history, source, diffusivity, target)))
@@ -463,15 +460,16 @@
         compiler_params=params,
     )(got)
     solved = lax.all_to_all(back, AXIS, split_axis=0, concat_axis=0, tiled=True)
-    return pl.pallas_call(
+    update, totals = pl.pallas_call(
         final_kernel,
         name="final",
-        out_shape=[shape((ROWS, NY), F32), shape((2,), F32)],
+        out_shape=[shape((VREGS * SUB, LANES), F32), shape((2,), F32)],
         in_specs=[vmem] * 4,
         out_specs=[vmem, pl.BlockSpec(memory_space=pltpu.SMEM)],
-        scratch_shapes=[tiles],
         compiler_params=params,
     )(solved, part, above, below)
+    update = update.reshape(HALVES, TILES, SUB, LANES).transpose(0, 2, 1, 3).reshape(ROWS, NY)
+    return update, totals
 
 
 def solution(mesh):

time: 43.5 us -> 43.4 us (level)
  no operation moved by 1% of the time
where the time goes in v7:
time: 43.4 us; the launch traced here: 43.3 us
  blocking collectives  36.1 us (83%)
  Pallas kernels  6.52 us (15%)
  between operations  0.64 us (1%)
    all_to_all x1, blocking collectives, body(): lax.all_to_all(msg.reshape(BLOCKS, 4, LANES), AXIS, split_axis=0, concat_...  22.2 us
    all_to_all x1, blocking collectives, body(): solved = lax.all_to_all(back, AXIS, split_axis=0, concat_axis=0, tiled=True)  14 us
    pallas_call x1, Pallas kernels, body(): pl.pallas_call(local_kernel, name='local', out_shape=[shape((4 * BLOCKS,...  5.11 us

profile of v7, /device:TPU:1, one launch (start us, length us, event | category | flops | bytes accessed | tf_op | source)
XLA Modules:
  0.0 43.3 jit_solution(4739209972532012735)
XLA Ops:
  0.6 5.1 %local.1 = (f32[512,128]{1,0:T(8,128)S(1)}, f32[480,128]{1,0:T(8,128)S(1)}, f32[480,128]{1,0:T(8,128)S(1)}, f32[480,128]{1,0:T(8,128)S(1)}) custom-call(f32[32,16,4096]{2,1,0:T(8,128)} %hist_hbm.1, f32[16,4096]{1,0:T(8,128)} %src_hbm.1, f32[16,4096]{1,0:T(8,128)} %dif_hbm.1, f32[16,4096]{1,0:T(8,128)} %tgt_hbm.1), custom_call_target="tpu_custom_call" | custom-call | tf_op jit(solution)/shard_map/local/pallas_call | solution.py:435
  5.7 22.2 %all_to_all.16 = f32[128,4,128]{2,1,0:T(4,128)S(1)} all-to-all(f32[128,4,128]{2,1,0:T(4,128)S(1)} %bitcast.14), channel_id=1, replica_groups=mesh['rows'=128] {'rows'}, dimensions={0} | all-to-all | bytes 524288 | tf_op jit(solution)/shard_map/all_to_all | solution.py:450
  27.9 0.6 %reduced.1 = f32[128,128]{1,0:T(8,128)S(1)} custom-call(f32[512,128]{1,0:T(8,128)S(1)} %bitcast.11), custom_call_target="tpu_custom_call" | custom-call | tf_op jit(solution)/shard_map/reduced/pallas_call | solution.py:453
  28.5 14.0 %all_to_all.17 = f32[128,1,128]{2,1,0:T(1,128)S(1)} all-to-all(f32[128,1,128]{2,1,0:T(1,128)S(1)} %bitcast.13), channel_id=1, replica_groups=mesh['rows'=128] {'rows'}, dimensions={0} | all-to-all | bytes 131072 | tf_op jit(solution)/shard_map/all_to_all | solution.py:462
  42.5 0.8 %final.1 = (f32[512,128]{1,0:T(8,128)}, f32[2]{0:T(128)}) custom-call(f32[128,128]{1,0:T(8,128)S(1)} %bitcast.12, f32[480,128]{1,0:T(8,128)S(1)} %get-tuple-element.9.part, f32[480,128]{1,0:T(8,128)S(1)} %get-tuple-element.10.above, f32[480,128]{1,0:T(8,128)S(1)} %get-tuple-element.11.below), custom_call_target="tpu_custom_call" | custom-call | tf_op jit(solution)/shard_map/final/pallas_call | solution.py:463

commit v8 on v7

--- a/solution.py
+++ b/solution.py
@@ -85,7 +85,7 @@
     msg, part, above, below,
     hist, src, dif, tgt,
     couple, inv, main, upper, beyond, first, centre, rhs,
-    dif_l, tgt_l, sw_l, gg, hh, rr, pp,
+    sw_l, gg, hh, rr, pp,
     weights, sems,
 ):
     def piece(h, k, sem):
@@ -113,8 +113,7 @@
     copies[0].wait()
     for h in range(HALVES):
         for t in range(TILES):
-            c = STIFF * dif[h * SUB:(h + 1) * SUB, t * LANES:(t + 1) * LANES]
-            dif_l[tile(h, t), :] = c
+            c = STIFF * dif[tile(h, t), :]
             q = 1.0 / c
             first[tile(h, t), :] = q
             u = 0.5 * q * (1.0 / (2.0 + q))
@@ -123,7 +122,7 @@
 
     g = h_ = None
     for r in range(ROWS):
-        c = dif_l[line(r), :]
+        c = STIFF * dif[line(r), :]
         if r == 0:
             q = 1.0 / (1.0 + 2.0 * c)
             g = c * q
@@ -305,10 +304,6 @@
     for h in range(HALVES):
         if h == HALVES - 1:
             copies[2].wait()
-            for i in range(VREGS):
-                g = i // TILES
-                t = i % TILES
-                tgt_l[tile(g, t), :] = tgt[g * SUB:(g + 1) * SUB, t * LANES:(t + 1) * LANES]
         for c in range(TILES // CHUNK_TILES):
             if c * CHUNK_TILES in PIECES[h]:
                 pieces[h][PIECES[h].index(c * CHUNK_TILES)].wait()
@@ -319,7 +314,7 @@
             p = s if r == 0 else s + gg[wide(r), :] * p
             pp[wide(r), :] = p
     tip = p
-    d = tgt_l[line(INNER), :]
+    d = tgt[line(INNER), :]
     sum_dd = d * d
     sum_db = -d
     sum_da = zero
@@ -331,7 +326,7 @@
         part[wide(r), :] = p
         a = above[wide(r), :]
         b = below[wide(r), :]
-        d = p - tgt_l[line(r), :]
+        d = p - tgt[line(r), :]
         sum_p = sum_p + p
         sum_dd = sum_dd + d * d
         sum_da = sum_da + d * a
@@ -421,6 +416,10 @@
     update[line(INNER), :] = z
 
 
+def by_tile(x):
+    return x.reshape(HALVES, SUB, TILES, LANES).transpose(0, 2, 1, 3).reshape(VREGS * SUB, LANES)
+
+
 def body(history, source, diffusivity, target):
     anywhere = pl.BlockSpec(memory_space=pltpu.HBM)
     vmem = pl.BlockSpec(memory_space=pltpu.VMEM)
@@ -439,14 +438,14 @@
         in_specs=[anywhere] * 4,
         out_specs=[vmem] * 4,
         scratch_shapes=[
-            pltpu.VMEM((LEVELS, ROWS, NY), F32), block, block, block,
+            pltpu.VMEM((LEVELS, ROWS, NY), F32), block, tiles, tiles,
             stages, stages, pair, tiles, tiles, tiles, block_tile, pair,
-            tiles, tiles, tiles, tiles, tiles, tiles, tiles,
+            tiles, tiles, tiles, tiles, tiles,
             pltpu.VMEM((LEVELS * SUB, LANES), F32),
             pltpu.SemaphoreType.DMA((COPIES,)),
         ],
         compiler_params=params,
-    )(*(pltpu.with_memory_space_constraint(x, pltpu.HBM) for x in (history, source, diffusivity, target)))
+    )(*(pltpu.with_memory_space_constraint(x, pltpu.HBM) for x in (history, source, by_tile(diffusivity), by_tile(target))))
     got = lax.all_to_all(
         msg.reshape(BLOCKS, 4, LANES), AXIS, split_axis=0, concat_axis=0, tiled=True
     ).reshape(4 * BLOCKS, LANES)

time: 43.4 us -> 43.4 us (level)
  no operation moved by 1% of the time
where the time goes in v8:
time: 43.4 us; the launch traced here: 43.3 us
  blocking collectives  36.1 us (83%)
  Pallas kernels  6.5 us (15%)
  between operations  0.64 us (1%)
    all_to_all x1, blocking collectives, body(): lax.all_to_all(msg.reshape(BLOCKS, 4, LANES), AXIS, split_axis=0, concat_...  22.2 us
    all_to_all x1, blocking collectives, body(): solved = lax.all_to_all(back, AXIS, split_axis=0, concat_axis=0, tiled=True)  14 us
    pallas_call x1, Pallas kernels, body(): pl.pallas_call(local_kernel, name='local', out_shape=[shape((4 * BLOCKS,...  5.09 us

profile of v8, /device:TPU:1, one launch (start us, length us, event | category | flops | bytes accessed | tf_op | source)
XLA Modules:
  0.0 43.3 jit_solution(12426335543061204816)
XLA Ops:
  0.6 5.1 %local.1 = (f32[512,128]{1,0:T(8,128)S(1)}, f32[480,128]{1,0:T(8,128)S(1)}, f32[480,128]{1,0:T(8,128)S(1)}, f32[480,128]{1,0:T(8,128)S(1)}) custom-call(f32[32,16,4096]{2,1,0:T(8,128)} %hist_hbm.1, f32[16,4096]{1,0:T(8,128)} %src_hbm.1, f32[512,128]{1,0:T(8,128)} %bitcast.25, f32[512,128]{1,0:T(8,128)} %bitcast.26), custom_call_target="tpu_custom_call" | custom-call | tf_op jit(solution)/shard_map/local/pallas_call | solution.py:434
  5.7 22.2 %all_to_all.16 = f32[128,4,128]{2,1,0:T(4,128)S(1)} all-to-all(f32[128,4,128]{2,1,0:T(4,128)S(1)} %bitcast.24), channel_id=1, replica_groups=mesh['rows'=128] {'rows'}, dimensions={0} | all-to-all | bytes 524288 | tf_op jit(solution)/shard_map/all_to_all | solution.py:449
  27.9 0.6 %reduced.1 = f32[128,128]{1,0:T(8,128)S(1)} custom-call(f32[512,128]{1,0:T(8,128)S(1)} %bitcast.21), custom_call_target="tpu_custom_call" | custom-call | tf_op jit(solution)/shard_map/reduced/pallas_call | solution.py:452
  28.5 14.0 %all_to_all.17 = f32[128,1,128]{2,1,0:T(1,128)S(1)} all-to-all(f32[128,1,128]{2,1,0:T(1,128)S(1)} %bitcast.23), channel_id=1, replica_groups=mesh['rows'=128] {'rows'}, dimensions={0} | all-to-all | bytes 131072 | tf_op jit(solution)/shard_map/all_to_all | solution.py:461
  42.4 0.8 %final.1 = (f32[512,128]{1,0:T(8,128)}, f32[2]{0:T(128)}) custom-call(f32[128,128]{1,0:T(8,128)S(1)} %bitcast.22, f32[480,128]{1,0:T(8,128)S(1)} %get-tuple-element.9.part, f32[480,128]{1,0:T(8,128)S(1)} %get-tuple-element.10.above, f32[480,128]{1,0:T(8,128)S(1)} %get-tuple-element.11.below), custom_call_target="tpu_custom_call" | custom-call | tf_op jit(solution)/shard_map/final/pallas_call | solution.py:462

commit v9 on v7

--- a/solution.py
+++ b/solution.py
@@ -20,7 +20,7 @@
 BLOCKS = 128
 INNER = ROWS - 1
 CHUNK_TILES = 8
-PIECES = ((0, 16, 32), (0, 16, 32))
+PIECES = ((0, 32), (0, 16, 32))
 COPIES = 3 + sum(len(cuts) - 1 for cuts in PIECES)
 STEPS = 7
 MID = TILES // 2

time: 43.4 us -> 43.5 us (level)
  no operation moved by 1% of the time
where the time goes in v9:
time: 43.5 us; the launch traced here: 43.4 us
  blocking collectives  36.1 us (83%)
  Pallas kernels  6.57 us (15%)
  between operations  0.64 us (1%)
    all_to_all x1, blocking collectives, body(): lax.all_to_all(msg.reshape(BLOCKS, 4, LANES), AXIS, split_axis=0, concat_...  22.2 us
    all_to_all x1, blocking collectives, body(): solved = lax.all_to_all(back, AXIS, split_axis=0, concat_axis=0, tiled=True)  14 us
    pallas_call x1, Pallas kernels, body(): pl.pallas_call(local_kernel, name='local', out_shape=[shape((4 * BLOCKS,...  5.16 us

profile of v9, /device:TPU:1, one launch (start us, length us, event | category | flops | bytes accessed | tf_op | source)
XLA Modules:
  0.0 43.4 jit_solution(10439403529175654082)
XLA Ops:
  0.6 5.2 %local.1 = (f32[512,128]{1,0:T(8,128)S(1)}, f32[480,128]{1,0:T(8,128)S(1)}, f32[480,128]{1,0:T(8,128)S(1)}, f32[480,128]{1,0:T(8,128)S(1)}) custom-call(f32[32,16,4096]{2,1,0:T(8,128)} %hist_hbm.1, f32[16,4096]{1,0:T(8,128)} %src_hbm.1, f32[16,4096]{1,0:T(8,128)} %dif_hbm.1, f32[16,4096]{1,0:T(8,128)} %tgt_hbm.1), custom_call_target="tpu_custom_call" | custom-call | tf_op jit(solution)/shard_map/local/pallas_call | solution.py:435
  5.8 22.2 %all_to_all.16 = f32[128,4,128]{2,1,0:T(4,128)S(1)} all-to-all(f32[128,4,128]{2,1,0:T(4,128)S(1)} %bitcast.14), channel_id=1, replica_groups=mesh['rows'=128] {'rows'}, dimensions={0} | all-to-all | bytes 524288 | tf_op jit(solution)/shard_map/all_to_all | solution.py:450
  28.0 0.6 %reduced.1 = f32[128,128]{1,0:T(8,128)S(1)} custom-call(f32[512,128]{1,0:T(8,128)S(1)} %bitcast.11), custom_call_target="tpu_custom_call" | custom-call | tf_op jit(solution)/shard_map/reduced/pallas_call | solution.py:453
  28.5 14.0 %all_to_all.17 = f32[128,1,128]{2,1,0:T(1,128)S(1)} all-to-all(f32[128,1,128]{2,1,0:T(1,128)S(1)} %bitcast.13), channel_id=1, replica_groups=mesh['rows'=128] {'rows'}, dimensions={0} | all-to-all | bytes 131072 | tf_op jit(solution)/shard_map/all_to_all | solution.py:462
  42.5 0.8 %final.1 = (f32[512,128]{1,0:T(8,128)}, f32[2]{0:T(128)}) custom-call(f32[128,128]{1,0:T(8,128)S(1)} %bitcast.12, f32[480,128]{1,0:T(8,128)S(1)} %get-tuple-element.9.part, f32[480,128]{1,0:T(8,128)S(1)} %get-tuple-element.10.above, f32[480,128]{1,0:T(8,128)S(1)} %get-tuple-element.11.below), custom_call_target="tpu_custom_call" | custom-call | tf_op jit(solution)/shard_map/final/pallas_call | solution.py:463
